TPU v7x, 32 devices: a whole 2x2x4 slice. The times are simulated.
32 devices in a mesh: grp: 2 (over x), tp: 4 (over y, core), pp: 4 (over z).
Axes of the slice: x: 2, y: 2, z: 4, core: 2. Of those that a mesh axis runs over, the one named last changes fastest.
Arguments:
- tokens: bfloat16 [1024, 8192], P('grp', 'tp'), parts along dimension 0, may hold values from -12 to 12
- gain: bfloat16 [4, 8192], P('pp', 'tp'), may hold values from 0.099609375 to 1.8984375
- q_weight: bfloat16 [4, 8192, 4096], P('pp', None, 'tp'), may hold values from -0.5 to 0.5
- kv_weight: bfloat16 [4, 8192, 2048], P('pp', None, 'tp'), may hold values from -0.5 to 0.5
- out_weight: bfloat16 [4, 4096, 8192], P('pp', None, 'tp'), may hold values from -0.09375 to 0.09375
- page_table: int32 [4, 8, 128], P('pp'), may hold values from 0 to 1023, as said below
- segment_ids: int32 [1024], P('grp'), parts along dimension 0, may hold values from 0 to 2, never falling along the last dimension, each value on 1 to 256 neighbouring positions
Outputs:
- hidden: bfloat16 [1024, 8192], P(('grp', 'pp'), 'tp'), parts along dimension 0
- kv_cache: bfloat16 [4, 2048, 4, 256], P('pp', ('grp', 'tp')), parts along dimension 1
There are 2 independent parts, one for each index of `grp`. A program takes and returns all parts, laid end to end along the dimension named above; an argument that names none is the same for every part. Nothing has to cross between parts.
Inputs may be any that keep to these rules, and one draw needn't show every extreme that they name: `page_table`: every entry of a layer's table is distinct and every one of the 1024 values occurs once. For each layer, head and micro-batch the 16 blocks form a run; in each run half of the devices receive exactly 8 pages and the others none, so each device receives exactly 256 pages of a layer.
All inputs are finite; a program needn't handle non-finite values.
Results may differ from a plain program's by a relative error of at most 0.017.
Values may be sent and summed in bfloat16 or wider, within the bound.
A program may use at most 128 MiB of HBM per device.

v0:
```python
import math

import jax
import jax.numpy as jnp
from jax import lax
from jax.sharding import PartitionSpec as P

MODEL_WIDTH = 8192
HEAD_SIZE = 128
KEY_VALUE_HEADS = 8
MB_TOK = 64
MICRO_BATCHES = 8
PAGE_TOKENS = 4


eps_norm = 1e-05


def partner_2(x, axis, apart):
    return lax.ppermute(x, axis, [(i, i ^ 1 << apart) for i in range(lax.axis_size(axis))])


def shifted(x, axis, by):
    peers = lax.axis_size(axis)
    pairs = [(i, i + by) for i in range(peers) if 0 <= i + by < peers]
    return lax.ppermute(x, axis, pairs)


def from_root(x, axis, root):
    mine = lax.axis_index(axis) == root
    return lax.psum(jnp.where(mine, x, jnp.zeros_like(x)), axis)


def send_pages(kv_own, page_rows, micro_idx, is_live, kv_cache, first_head, tensor_parallel_width):
    row_count = kv_own.shape[0]
    kv_cols = kv_own.shape[1]
    head_width = kv_cache.shape[2]
    cache_page_count = kv_cache.shape[0]
    held_heads = max(1, kv_cols // head_width)
    unit_cols = kv_cols // held_heads
    blocks = row_count // PAGE_TOKENS
    paged_rows = (
        kv_own.reshape(blocks, PAGE_TOKENS, held_heads, unit_cols)
        .transpose(2, 0, 1, 3)
        .reshape(held_heads * blocks, PAGE_TOKENS * unit_cols)
    )
    target_pages = lax.dynamic_slice(
        page_rows, (first_head, micro_idx * blocks), (held_heads, blocks)
    ).reshape(-1)
    device = target_pages // cache_page_count
    cache_page_index = target_pages % cache_page_count
    page_count = held_heads * blocks
    capacity = 2 * page_count // tensor_parallel_width
    onehot = (
        device[:, None] == jnp.arange(tensor_parallel_width, dtype=jnp.int32)[None, :]
    ).astype(jnp.int32)
    earlier = jnp.cumsum(onehot, axis=0) - onehot
    arrival = jnp.sum(earlier * onehot, axis=1)
    position = device * capacity + arrival
    outgoing = (
        jnp.zeros((tensor_parallel_width * capacity, PAGE_TOKENS * unit_cols), jnp.bfloat16)
        .at[position]
        .set(paged_rows)
    )
    labels = (
        jnp.full((tensor_parallel_width * capacity,), cache_page_count, jnp.int32)
        .at[position]
        .set(jnp.where(is_live, cache_page_index, cache_page_count))
    )
    incoming, landing = (
        lax.all_to_all(outgoing, "tp", split_axis=0, concat_axis=0, tiled=True),
        lax.all_to_all(labels, "tp", split_axis=0, concat_axis=0, tiled=True),
    )
    offsets = jnp.arange(tensor_parallel_width, dtype=jnp.int32) * kv_cols % head_width
    lane_ids = jnp.arange(head_width, dtype=jnp.int32)
    within = jnp.arange(unit_cols, dtype=jnp.int32)
    placer = (lane_ids[None, None, :] == offsets[:, None, None] + within[None, :, None]).astype(
        jnp.bfloat16
    )
    spread = jnp.einsum(
        "snw,swv->snv",
        incoming.reshape(tensor_parallel_width, capacity * PAGE_TOKENS, unit_cols),
        placer,
        preferred_element_type=jnp.float32,
    ).astype(jnp.bfloat16)
    return kv_cache.at[landing].add(
        spread.reshape(tensor_parallel_width * capacity, PAGE_TOKENS, head_width), mode="drop"
    )


def body(tokens, gain, q_weight, kv_weight, out_weight, page_table, segment_ids):
    tensor_parallel_width = lax.axis_size("tp")
    pp_size = lax.axis_size("pp")
    tp_rank = lax.axis_index("tp")
    section_idx = lax.axis_index("pp")
    w_query = q_weight[0]
    w_keyval = kv_weight[0]
    w_output = out_weight[0]
    page_rows = page_table[0]
    local_width = tokens.shape[1]
    row_total = tokens.shape[0]
    row_count = MB_TOK
    head_dim = HEAD_SIZE
    kv_cols = w_keyval.shape[1]
    held_heads = max(1, kv_cols // (2 * head_dim))
    q_heads = w_query.shape[1] // head_dim
    per_kv = q_heads // held_heads
    first_head = tp_rank * kv_cols // (2 * head_dim)
    cache_page_count = KEY_VALUE_HEADS * (row_total // PAGE_TOKENS) // tensor_parallel_width
    score_scale = 1.0 / math.sqrt(head_dim)
    step_count = MICRO_BATCHES + pp_size - 1
    key_pos = jnp.arange(row_total, dtype=jnp.int32)

    def add_columns(block_cols):
        return (
            jnp.dot(block_cols, w_query, preferred_element_type=jnp.float32),
            jnp.dot(block_cols, w_keyval, preferred_element_type=jnp.float32),
        )

    def add_outputs(block_cols):
        return jnp.dot(block_cols, w_output, preferred_element_type=jnp.float32)

    def one_step(step_idx, state_tuple):
        received, kv_buffer, kv_cache, collected = state_tuple
        micro_raw = step_idx - section_idx
        is_live = (micro_raw >= 0) & (micro_raw < MICRO_BATCHES)
        micro_idx = jnp.clip(micro_raw, 0, MICRO_BATCHES - 1)
        row_start = micro_idx * row_count
        first_rows = lax.dynamic_slice_in_dim(tokens, row_start, row_count, 0)
        current = jnp.where(section_idx == 0, first_rows, received)
        widened = current.astype(jnp.float32)
        partial_sq = jnp.sum(widened * widened, axis=1, keepdims=True)
        mean_sq = lax.psum(partial_sq, "tp") / MODEL_WIDTH
        normed = (widened * lax.rsqrt(mean_sq + eps_norm) * gain.astype(jnp.float32)).astype(
            jnp.bfloat16
        )
        query_sum, keyval_sum = add_columns(lax.all_gather(normed, "tp", axis=1, tiled=True))
        query_matrix = query_sum.astype(jnp.bfloat16)
        kv_own = keyval_sum.astype(jnp.bfloat16)
        if tensor_parallel_width > KEY_VALUE_HEADS:
            partner = partner_2(kv_own, "tp", 0)
            first_half = tp_rank % 2 == 0
            head_pair = jnp.where(
                first_half,
                jnp.concatenate([kv_own, partner], axis=1),
                jnp.concatenate([partner, kv_own], axis=1),
            )
        else:
            head_pair = kv_own
        kv_cache = send_pages(
            kv_own, page_rows, micro_idx, is_live, kv_cache, first_head, tensor_parallel_width
        )
        refreshed = lax.dynamic_update_slice_in_dim(kv_buffer, head_pair, row_start, 0)
        kv_buffer = jnp.where(is_live, refreshed, kv_buffer)
        kv_view = kv_buffer.reshape(row_total, held_heads, 2, head_dim)
        grouped_queries = query_matrix.reshape(row_count, held_heads, per_kv, head_dim)
        scores = (
            jnp.einsum(
                "qgpd,kgd->gpqk",
                grouped_queries,
                kv_view[:, :, 0],
                preferred_element_type=jnp.float32,
            )
            * score_scale
        )
        query_pos = row_start + jnp.arange(row_count, dtype=jnp.int32)
        seg_query = lax.dynamic_slice_in_dim(segment_ids, row_start, row_count, 0)
        allowed = (key_pos[None, :] <= query_pos[:, None]) & (
            segment_ids[None, :] == seg_query[:, None]
        )
        scores = jnp.where(allowed[None, None], scores, -1e30)
        row_max = jnp.max(scores, axis=-1, keepdims=True)
        raised = jnp.exp(scores - row_max)
        weights = (raised / jnp.sum(raised, axis=-1, keepdims=True)).astype(jnp.bfloat16)
        attended = jnp.einsum(
            "gpqk,kgd->qgpd", weights, kv_view[:, :, 1], preferred_element_type=jnp.float32
        )
        attended = attended.astype(jnp.bfloat16).reshape(row_count, q_heads * head_dim)
        projected = add_outputs(lax.all_gather(attended, "tp", axis=1, tiled=True))
        produced = (widened + projected).astype(jnp.bfloat16)
        placed = lax.dynamic_update_slice_in_dim(collected, produced, row_start, 0)
        collected = jnp.where(is_live & (section_idx == pp_size - 1), placed, collected)
        handed = shifted(produced, "pp", 1)
        return (handed, kv_buffer, kv_cache, collected)

    initial = (
        jnp.zeros((row_count, local_width), jnp.bfloat16),
        jnp.zeros((row_total, held_heads * 2 * head_dim), jnp.bfloat16),
        jnp.zeros((cache_page_count, PAGE_TOKENS, 2 * head_dim), jnp.bfloat16),
        jnp.zeros((row_total, local_width), jnp.bfloat16),
    )
    finished = lax.fori_loop(0, step_count, one_step, initial)
    whole_final = from_root(finished[3], "pp", pp_size - 1)
    share_rows = row_total // pp_size
    hidden = lax.dynamic_slice_in_dim(whole_final, section_idx * share_rows, share_rows, 0)
    return (hidden, finished[2][None])


def solution(mesh):
    placed = (
        P("grp", "tp"),
        P("pp", "tp"),
        P("pp", None, "tp"),
        P("pp", None, "tp"),
        P("pp", None, "tp"),
        P("pp", None, None),
        P("grp"),
    )
    return jax.shard_map(
        body,
        mesh=mesh,
        in_specs=placed,
        out_specs=(P(("grp", "pp"), "tp"), P("pp", ("grp", "tp"), None, None)),
        check_vma=False,
    )
```

profile of v0, /device:TPU:0, one launch (start us, length us, event | category | flops | bytes accessed | tf_op | source)
XLA Modules:
  0.0 928.2 jit_solution(15119671289388943089)
XLA Ops:
  9.8 821.5 %while.22 = (s32[]{:T(128)}, bf16[64,2048]{1,0:T(8,128)(2,1)S(1)}, bf16[512,512]{1,0:T(8,128)(2,1)S(1)}, bf16[256,4,256]{2,1,0:T(4,128)(2,1)S(1)}, bf16[512,2048...) while((s32[]{:T(128)}, bf16[64,2048]{1,0:T(8,128)(2,1)S(1)}, ...), condition=%wide.region_10.11_spmd.clone, body=%wide.region_0.10_spmd.clone.sunk | while | flops 2923866880 | bytes 66799608 | solution.py:192
  11.1 8.4 psum.24
  31.1 6.4 all-gather.2.cloned.1.call-done
  37.5 5.3 dynamic-slice_select_fusion.4
  43.0 8.8 convolution_convert_fusion.6
  54.5 7.2 all_gather.25
  61.6 9.6 %select_dynamic-update-slice_fusion.2 = (bf16[512,2048]{1,0:T(8,128)(2,1)}, bf16[64,2048]{1,0:T(8,128)(2,1)S(1)}) fusion(bf16[512,2048]{1,0:T(8,128)(2,1)} %get-tuple-element.624, s32[]{:T(128)S(6)} %select_n.328, pred[]{:T(512)S(6)} %and.146, bf16[64,4096]{1,0:T(8,128)(2,1)S(1)} %all_gather.25, bf16[4096,2048]{1,0:T(8,128)(2,1)} %get-tuple-element.658, ...), kind=kOutput, calls=%fused_computation.27.clone.1 | convolution fusion | flops 1074266112 | bytes 18350084 | tf_op jit(solution)/shard_map/while/body/eval_jaxpr/dot_general | solution.py:121
  88.7 5.8 psum.24
  106.2 5.6 all-gather.2.cloned.1.call-done
  111.8 5.3 dynamic-slice_select_fusion.4
  117.3 8.8 convolution_convert_fusion.6
  129.2 7.2 all_gather.25
  136.3 9.5 %select_dynamic-update-slice_fusion.2 = (bf16[512,2048]{1,0:T(8,128)(2,1)}, bf16[64,2048]{1,0:T(8,128)(2,1)S(1)}) fusion(bf16[512,2048]{1,0:T(8,128)(2,1)} %get-tuple-element.624, s32[]{:T(128)S(6)} %select_n.328, pred[]{:T(512)S(6)} %and.146, bf16[64,4096]{1,0:T(8,128)(2,1)S(1)} %all_gather.25, bf16[4096,2048]{1,0:T(8,128)(2,1)} %get-tuple-element.658, ...), kind=kOutput, calls=%fused_computation.27.clone.1 | convolution fusion | flops 1074266112 | bytes 18350084 | tf_op jit(solution)/shard_map/while/body/eval_jaxpr/dot_general | solution.py:121
  163.0 5.8 psum.24
  180.5 5.6 all-gather.2.cloned.1.call-done
  186.1 5.3 dynamic-slice_select_fusion.4
  191.6 8.8 convolution_convert_fusion.6
  203.0 7.2 all_gather.25
  210.2 9.5 %select_dynamic-update-slice_fusion.2 = (bf16[512,2048]{1,0:T(8,128)(2,1)}, bf16[64,2048]{1,0:T(8,128)(2,1)S(1)}) fusion(bf16[512,2048]{1,0:T(8,128)(2,1)} %get-tuple-element.624, s32[]{:T(128)S(6)} %select_n.328, pred[]{:T(512)S(6)} %and.146, bf16[64,4096]{1,0:T(8,128)(2,1)S(1)} %all_gather.25, bf16[4096,2048]{1,0:T(8,128)(2,1)} %get-tuple-element.658, ...), kind=kOutput, calls=%fused_computation.27.clone.1 | convolution fusion | flops 1074266112 | bytes 18350084 | tf_op jit(solution)/shard_map/while/body/eval_jaxpr/dot_general | solution.py:121
  237.6 5.8 psum.24
  260.3 5.3 dynamic-slice_select_fusion.4
  265.8 8.8 convolution_convert_fusion.6
  277.7 7.2 all_gather.25
  284.8 9.5 %select_dynamic-update-slice_fusion.2 = (bf16[512,2048]{1,0:T(8,128)(2,1)}, bf16[64,2048]{1,0:T(8,128)(2,1)S(1)}) fusion(bf16[512,2048]{1,0:T(8,128)(2,1)} %get-tuple-element.624, s32[]{:T(128)S(6)} %select_n.328, pred[]{:T(512)S(6)} %and.146, bf16[64,4096]{1,0:T(8,128)(2,1)S(1)} %all_gather.25, bf16[4096,2048]{1,0:T(8,128)(2,1)} %get-tuple-element.658, ...), kind=kOutput, calls=%fused_computation.27.clone.1 | convolution fusion | flops 1074266112 | bytes 18350084 | tf_op jit(solution)/shard_map/while/body/eval_jaxpr/dot_general | solution.py:121
  311.5 5.8 psum.24
  329.0 5.6 all-gather.2.cloned.1.call-done
  334.5 5.3 dynamic-slice_select_fusion.4
  340.0 8.8 convolution_convert_fusion.6
  351.5 7.1 all_gather.25
  358.6 9.5 %select_dynamic-update-slice_fusion.2 = (bf16[512,2048]{1,0:T(8,128)(2,1)}, bf16[64,2048]{1,0:T(8,128)(2,1)S(1)}) fusion(bf16[512,2048]{1,0:T(8,128)(2,1)} %get-tuple-element.624, s32[]{:T(128)S(6)} %select_n.328, pred[]{:T(512)S(6)} %and.146, bf16[64,4096]{1,0:T(8,128)(2,1)S(1)} %all_gather.25, bf16[4096,2048]{1,0:T(8,128)(2,1)} %get-tuple-element.658, ...), kind=kOutput, calls=%fused_computation.27.clone.1 | convolution fusion | flops 1074266112 | bytes 18350084 | tf_op jit(solution)/shard_map/while/body/eval_jaxpr/dot_general | solution.py:121
  386.1 5.8 psum.24
  403.6 5.5 all-gather.2.cloned.1.call-done
  409.2 5.3 dynamic-slice_select_fusion.4
  414.6 8.8 convolution_convert_fusion.6
  426.5 7.2 all_gather.25
  433.7 9.5 %select_dynamic-update-slice_fusion.2 = (bf16[512,2048]{1,0:T(8,128)(2,1)}, bf16[64,2048]{1,0:T(8,128)(2,1)S(1)}) fusion(bf16[512,2048]{1,0:T(8,128)(2,1)} %get-tuple-element.624, s32[]{:T(128)S(6)} %select_n.328, pred[]{:T(512)S(6)} %and.146, bf16[64,4096]{1,0:T(8,128)(2,1)S(1)} %all_gather.25, bf16[4096,2048]{1,0:T(8,128)(2,1)} %get-tuple-element.658, ...), kind=kOutput, calls=%fused_computation.27.clone.1 | convolution fusion | flops 1074266112 | bytes 18350084 | tf_op jit(solution)/shard_map/while/body/eval_jaxpr/dot_general | solution.py:121
  460.3 5.8 psum.24
  477.8 5.6 all-gather.2.cloned.1.call-done
  483.3 5.3 dynamic-slice_select_fusion.4
  488.8 8.8 convolution_convert_fusion.6
  500.2 7.2 all_gather.25
  507.4 9.5 %select_dynamic-update-slice_fusion.2 = (bf16[512,2048]{1,0:T(8,128)(2,1)}, bf16[64,2048]{1,0:T(8,128)(2,1)S(1)}) fusion(bf16[512,2048]{1,0:T(8,128)(2,1)} %get-tuple-element.624, s32[]{:T(128)S(6)} %select_n.328, pred[]{:T(512)S(6)} %and.146, bf16[64,4096]{1,0:T(8,128)(2,1)S(1)} %all_gather.25, bf16[4096,2048]{1,0:T(8,128)(2,1)} %get-tuple-element.658, ...), kind=kOutput, calls=%fused_computation.27.clone.1 | convolution fusion | flops 1074266112 | bytes 18350084 | tf_op jit(solution)/shard_map/while/body/eval_jaxpr/dot_general | solution.py:121
  534.9 5.8 psum.24
  552.4 5.6 all-gather.2.cloned.1.call-done
  558.0 5.3 dynamic-slice_select_fusion.4
  563.4 8.8 convolution_convert_fusion.6
  575.2 7.2 all_gather.25
  582.4 9.5 %select_dynamic-update-slice_fusion.2 = (bf16[512,2048]{1,0:T(8,128)(2,1)}, bf16[64,2048]{1,0:T(8,128)(2,1)S(1)}) fusion(bf16[512,2048]{1,0:T(8,128)(2,1)} %get-tuple-element.624, s32[]{:T(128)S(6)} %select_n.328, pred[]{:T(512)S(6)} %and.146, bf16[64,4096]{1,0:T(8,128)(2,1)S(1)} %all_gather.25, bf16[4096,2048]{1,0:T(8,128)(2,1)} %get-tuple-element.658, ...), kind=kOutput, calls=%fused_computation.27.clone.1 | convolution fusion | flops 1074266112 | bytes 18350084 | tf_op jit(solution)/shard_map/while/body/eval_jaxpr/dot_general | solution.py:121
  609.0 5.8 psum.24
  626.5 5.7 all-gather.2.cloned.1.call-done
  632.2 5.3 dynamic-slice_select_fusion.4
  637.6 8.8 convolution_convert_fusion.6
  649.4 7.2 all_gather.25
  656.6 9.5 %select_dynamic-update-slice_fusion.2 = (bf16[512,2048]{1,0:T(8,128)(2,1)}, bf16[64,2048]{1,0:T(8,128)(2,1)S(1)}) fusion(bf16[512,2048]{1,0:T(8,128)(2,1)} %get-tuple-element.624, s32[]{:T(128)S(6)} %select_n.328, pred[]{:T(512)S(6)} %and.146, bf16[64,4096]{1,0:T(8,128)(2,1)S(1)} %all_gather.25, bf16[4096,2048]{1,0:T(8,128)(2,1)} %get-tuple-element.658, ...), kind=kOutput, calls=%fused_computation.27.clone.1 | convolution fusion | flops 1074266112 | bytes 18350084 | tf_op jit(solution)/shard_map/while/body/eval_jaxpr/dot_general | solution.py:121
  683.7 5.8 psum.24
  701.2 5.6 all-gather.2.cloned.1.call-done
  712.3 8.8 convolution_convert_fusion.6
  724.1 7.2 all_gather.25
  731.2 9.5 %select_dynamic-update-slice_fusion.2 = (bf16[512,2048]{1,0:T(8,128)(2,1)}, bf16[64,2048]{1,0:T(8,128)(2,1)S(1)}) fusion(bf16[512,2048]{1,0:T(8,128)(2,1)} %get-tuple-element.624, s32[]{:T(128)S(6)} %select_n.328, pred[]{:T(512)S(6)} %and.146, bf16[64,4096]{1,0:T(8,128)(2,1)S(1)} %all_gather.25, bf16[4096,2048]{1,0:T(8,128)(2,1)} %get-tuple-element.658, ...), kind=kOutput, calls=%fused_computation.27.clone.1 | convolution fusion | flops 1074266112 | bytes 18350084 | tf_op jit(solution)/shard_map/while/body/eval_jaxpr/dot_general | solution.py:121
  758.4 5.8 psum.24
  786.4 8.8 convolution_convert_fusion.6
  798.2 7.1 all_gather.25
  805.4 9.5 %select_dynamic-update-slice_fusion.2 = (bf16[512,2048]{1,0:T(8,128)(2,1)}, bf16[64,2048]{1,0:T(8,128)(2,1)S(1)}) fusion(bf16[512,2048]{1,0:T(8,128)(2,1)} %get-tuple-element.624, s32[]{:T(128)S(6)} %select_n.328, pred[]{:T(512)S(6)} %and.146, bf16[64,4096]{1,0:T(8,128)(2,1)S(1)} %all_gather.25, bf16[4096,2048]{1,0:T(8,128)(2,1)} %get-tuple-element.658, ...), kind=kOutput, calls=%fused_computation.27.clone.1 | convolution fusion | flops 1074266112 | bytes 18350084 | tf_op jit(solution)/shard_map/while/body/eval_jaxpr/dot_general | solution.py:121
  832.9 86.3 %all-reduce.2.cloned.1.call-done = bf16[512,2048]{1,0:T(8,128)(2,1)} async-done(((bf16[512,2048]{1,0:T(8,128)(2,1)}), bf16[512,2048]{1,0:T(8,128)(2,1)}) %all-reduce.2.cloned.1.call-update) | async-done | bytes 2097168 | tf_op jit(solution)/shard_map/psum | solution.py:31
  (579 shorter events, 378.0 us)
Async XLA Ops:
  8.0 1.8 copy-start.2
  8.0 1.8 copy-start.3
  9.8 27.7 %all-gather.2.cloned.1.call-start = ((), (), s32[]{:S(2)}) async-start(), calls=%async_computation.3 | async-start | bytes 1310720 | tf_op jit(solution)/shard_map/while/body/eval_jaxpr/all_gather | solution.py:137
  23.0 6.9 all-to-all-start
  37.5 5.5 copy-start
  71.2 16.3 %collective-permute-start = (bf16[64,2048]{1,0:T(8,128)(2,1)S(1)}, bf16[64,2048]{1,0:T(8,128)(2,1)S(1)}, u32[]{:S(2)}, u32[]{:S(2)}) collective-permute-start(bf16[64,2048]{1,0:T(8,128)(2,1)S(1)} %get-tuple-element.589), channel_id=1, source_target_pairs={{0,1},{1,2},{2,3},{4,5},{5,6},{6,7},{8,9},{9,10},{10,11},{12,13},{... | collective-permute-start | bytes 786440 | tf_op jit(solution)/shard_map/while/body/eval_jaxpr/ppermute | solution.py:26
  76.0 7.9 all-to-all-start.1
  87.5 24.3 %all-gather.2.cloned.1.call-start = ((), (), s32[]{:S(2)}) async-start(), calls=%async_computation.3 | async-start | bytes 1310720 | tf_op jit(solution)/shard_map/while/body/eval_jaxpr/all_gather | solution.py:137
  98.0 6.9 all-to-all-start
  111.8 5.5 copy-start
  145.9 15.9 %collective-permute-start = (bf16[64,2048]{1,0:T(8,128)(2,1)S(1)}, bf16[64,2048]{1,0:T(8,128)(2,1)S(1)}, u32[]{:S(2)}, u32[]{:S(2)}) collective-permute-start(bf16[64,2048]{1,0:T(8,128)(2,1)S(1)} %get-tuple-element.589), channel_id=1, source_target_pairs={{0,1},{1,2},{2,3},{4,5},{5,6},{6,7},{8,9},{9,10},{10,11},{12,13},{... | collective-permute-start | bytes 786440 | tf_op jit(solution)/shard_map/while/body/eval_jaxpr/ppermute | solution.py:26
  150.3 7.9 all-to-all-start.1
  161.8 24.3 %all-gather.2.cloned.1.call-start = ((), (), s32[]{:S(2)}) async-start(), calls=%async_computation.3 | async-start | bytes 1310720 | tf_op jit(solution)/shard_map/while/body/eval_jaxpr/all_gather | solution.py:137
  172.3 6.9 all-to-all-start
  186.1 5.5 copy-start
  219.7 16.7 %collective-permute-start = (bf16[64,2048]{1,0:T(8,128)(2,1)S(1)}, bf16[64,2048]{1,0:T(8,128)(2,1)S(1)}, u32[]{:S(2)}, u32[]{:S(2)}) collective-permute-start(bf16[64,2048]{1,0:T(8,128)(2,1)S(1)} %get-tuple-element.589), channel_id=1, source_target_pairs={{0,1},{1,2},{2,3},{4,5},{5,6},{6,7},{8,9},{9,10},{10,11},{12,13},{... | collective-permute-start | bytes 786440 | tf_op jit(solution)/shard_map/while/body/eval_jaxpr/ppermute | solution.py:26
  225.0 7.9 all-to-all-start.1
  236.4 23.9 %all-gather.2.cloned.1.call-start = ((), (), s32[]{:S(2)}) async-start(), calls=%async_computation.3 | async-start | bytes 1310720 | tf_op jit(solution)/shard_map/while/body/eval_jaxpr/all_gather | solution.py:137
  247.0 6.9 all-to-all-start
  260.3 5.5 copy-start
  294.4 15.9 %collective-permute-start = (bf16[64,2048]{1,0:T(8,128)(2,1)S(1)}, bf16[64,2048]{1,0:T(8,128)(2,1)S(1)}, u32[]{:S(2)}, u32[]{:S(2)}) collective-permute-start(bf16[64,2048]{1,0:T(8,128)(2,1)S(1)} %get-tuple-element.589), channel_id=1, source_target_pairs={{0,1},{1,2},{2,3},{4,5},{5,6},{6,7},{8,9},{9,10},{10,11},{12,13},{... | collective-permute-start | bytes 786440 | tf_op jit(solution)/shard_map/while/body/eval_jaxpr/ppermute | solution.py:26
  298.8 7.9 all-to-all-start.1
  310.3 24.2 %all-gather.2.cloned.1.call-start = ((), (), s32[]{:S(2)}) async-start(), calls=%async_computation.3 | async-start | bytes 1310720 | tf_op jit(solution)/shard_map/while/body/eval_jaxpr/all_gather | solution.py:137
  320.8 6.9 all-to-all-start
  334.5 5.5 copy-start
  368.2 16.7 %collective-permute-start = (bf16[64,2048]{1,0:T(8,128)(2,1)S(1)}, bf16[64,2048]{1,0:T(8,128)(2,1)S(1)}, u32[]{:S(2)}, u32[]{:S(2)}) collective-permute-start(bf16[64,2048]{1,0:T(8,128)(2,1)S(1)} %get-tuple-element.589), channel_id=1, source_target_pairs={{0,1},{1,2},{2,3},{4,5},{5,6},{6,7},{8,9},{9,10},{10,11},{12,13},{... | collective-permute-start | bytes 786440 | tf_op jit(solution)/shard_map/while/body/eval_jaxpr/ppermute | solution.py:26
  373.5 7.9 all-to-all-start.1
  384.9 24.2 %all-gather.2.cloned.1.call-start = ((), (), s32[]{:S(2)}) async-start(), calls=%async_computation.3 | async-start | bytes 1310720 | tf_op jit(solution)/shard_map/while/body/eval_jaxpr/all_gather | solution.py:137
  395.5 6.9 all-to-all-start
  409.2 5.5 copy-start
  443.2 15.9 %collective-permute-start = (bf16[64,2048]{1,0:T(8,128)(2,1)S(1)}, bf16[64,2048]{1,0:T(8,128)(2,1)S(1)}, u32[]{:S(2)}, u32[]{:S(2)}) collective-permute-start(bf16[64,2048]{1,0:T(8,128)(2,1)S(1)} %get-tuple-element.589), channel_id=1, source_target_pairs={{0,1},{1,2},{2,3},{4,5},{5,6},{6,7},{8,9},{9,10},{10,11},{12,13},{... | collective-permute-start | bytes 786440 | tf_op jit(solution)/shard_map/while/body/eval_jaxpr/ppermute | solution.py:26
  447.6 7.9 all-to-all-start.1
  459.1 24.2 %all-gather.2.cloned.1.call-start = ((), (), s32[]{:S(2)}) async-start(), calls=%async_computation.3 | async-start | bytes 1310720 | tf_op jit(solution)/shard_map/while/body/eval_jaxpr/all_gather | solution.py:137
  469.6 6.9 all-to-all-start
  483.3 5.5 copy-start
  516.9 16.8 %collective-permute-start = (bf16[64,2048]{1,0:T(8,128)(2,1)S(1)}, bf16[64,2048]{1,0:T(8,128)(2,1)S(1)}, u32[]{:S(2)}, u32[]{:S(2)}) collective-permute-start(bf16[64,2048]{1,0:T(8,128)(2,1)S(1)} %get-tuple-element.589), channel_id=1, source_target_pairs={{0,1},{1,2},{2,3},{4,5},{5,6},{6,7},{8,9},{9,10},{10,11},{12,13},{... | collective-permute-start | bytes 786440 | tf_op jit(solution)/shard_map/while/body/eval_jaxpr/ppermute | solution.py:26
  522.2 7.9 all-to-all-start.1
  533.7 24.2 %all-gather.2.cloned.1.call-start = ((), (), s32[]{:S(2)}) async-start(), calls=%async_computation.3 | async-start | bytes 1310720 | tf_op jit(solution)/shard_map/while/body/eval_jaxpr/all_gather | solution.py:137
  544.2 6.9 all-to-all-start
  558.0 5.5 copy-start
  591.9 15.8 %collective-permute-start = (bf16[64,2048]{1,0:T(8,128)(2,1)S(1)}, bf16[64,2048]{1,0:T(8,128)(2,1)S(1)}, u32[]{:S(2)}, u32[]{:S(2)}) collective-permute-start(bf16[64,2048]{1,0:T(8,128)(2,1)S(1)} %get-tuple-element.589), channel_id=1, source_target_pairs={{0,1},{1,2},{2,3},{4,5},{5,6},{6,7},{8,9},{9,10},{10,11},{12,13},{... | collective-permute-start | bytes 786440 | tf_op jit(solution)/shard_map/while/body/eval_jaxpr/ppermute | solution.py:26
  596.3 7.9 all-to-all-start.1
  607.8 24.3 %all-gather.2.cloned.1.call-start = ((), (), s32[]{:S(2)}) async-start(), calls=%async_computation.3 | async-start | bytes 1310720 | tf_op jit(solution)/shard_map/while/body/eval_jaxpr/all_gather | solution.py:137
  618.3 6.9 all-to-all-start
  632.1 5.5 copy-start
  666.1 16.4 %collective-permute-start = (bf16[64,2048]{1,0:T(8,128)(2,1)S(1)}, bf16[64,2048]{1,0:T(8,128)(2,1)S(1)}, u32[]{:S(2)}, u32[]{:S(2)}) collective-permute-start(bf16[64,2048]{1,0:T(8,128)(2,1)S(1)} %get-tuple-element.589), channel_id=1, source_target_pairs={{0,1},{1,2},{2,3},{4,5},{5,6},{6,7},{8,9},{9,10},{10,11},{12,13},{... | collective-permute-start | bytes 786440 | tf_op jit(solution)/shard_map/while/body/eval_jaxpr/ppermute | solution.py:26
  671.0 7.9 all-to-all-start.1
  682.5 24.2 %all-gather.2.cloned.1.call-start = ((), (), s32[]{:S(2)}) async-start(), calls=%async_computation.3 | async-start | bytes 1310720 | tf_op jit(solution)/shard_map/while/body/eval_jaxpr/all_gather | solution.py:137
  693.0 6.9 all-to-all-start
  706.8 5.5 copy-start
  740.8 16.4 %collective-permute-start = (bf16[64,2048]{1,0:T(8,128)(2,1)S(1)}, bf16[64,2048]{1,0:T(8,128)(2,1)S(1)}, u32[]{:S(2)}, u32[]{:S(2)}) collective-permute-start(bf16[64,2048]{1,0:T(8,128)(2,1)S(1)} %get-tuple-element.589), channel_id=1, source_target_pairs={{0,1},{1,2},{2,3},{4,5},{5,6},{6,7},{8,9},{9,10},{10,11},{12,13},{... | collective-permute-start | bytes 786440 | tf_op jit(solution)/shard_map/while/body/eval_jaxpr/ppermute | solution.py:26
  745.6 7.9 all-to-all-start.1
  757.1 23.8 %all-gather.2.cloned.1.call-start = ((), (), s32[]{:S(2)}) async-start(), calls=%async_computation.3 | async-start | bytes 1310720 | tf_op jit(solution)/shard_map/while/body/eval_jaxpr/all_gather | solution.py:137
  767.6 6.9 all-to-all-start
  780.9 5.5 copy-start
  814.9 16.4 %collective-permute-start = (bf16[64,2048]{1,0:T(8,128)(2,1)S(1)}, bf16[64,2048]{1,0:T(8,128)(2,1)S(1)}, u32[]{:S(2)}, u32[]{:S(2)}) collective-permute-start(bf16[64,2048]{1,0:T(8,128)(2,1)S(1)} %get-tuple-element.589), channel_id=1, source_target_pairs={{0,1},{1,2},{2,3},{4,5},{5,6},{6,7},{8,9},{9,10},{10,11},{12,13},{... | collective-permute-start | bytes 786440 | tf_op jit(solution)/shard_map/while/body/eval_jaxpr/ppermute | solution.py:26
  819.7 7.9 all-to-all-start.1
  831.3 1.6 copy-start.1
  831.3 87.9 %all-reduce.2.cloned.1.call-start = ((), (), s32[]{:S(2)}) async-start(), calls=%async_computation.2 | async-start | bytes 4194304 | tf_op jit(solution)/shard_map/psum | solution.py:31
Sparse Core Ops, SparseCore 0:
  20.5 17.0 all-gather.1
  95.5 16.2 all-gather.1
  169.8 16.2 all-gather.1
  244.5 15.7 all-gather.1
  318.3 16.2 all-gather.1
  393.0 16.1 all-gather.1
  467.1 16.2 all-gather.1
  541.7 16.2 all-gather.1
  615.8 16.3 all-gather.1
  690.5 16.2 all-gather.1
  765.1 15.7 all-gather.1
Sparse Core Ops, SparseCore 1:
  834.1 85.0 all-reduce.1
where the time goes:
time: 932 us; the launch traced here: 928 us
  matrix products  285 us (31%)
  waiting for transfers between devices  231 us (25%)
  blocking collectives  145 us (16%)
  starting transfers between devices  109 us (12%)
  other arithmetic  70.3 us (8%)
  local copies, waits for them, and re-layouts  69.7 us (7%)
  between operations  15.2 us (2%)
    dot_general x11, matrix products, add_outputs(): return jnp.dot(block_cols, w_output, preferred_element_type=jnp.float32)  105 us
    dot_general x11, matrix products, add_columns(): jnp.dot(block_cols, w_query, preferred_element_type=jnp.float32)  96.7 us
    psum x1, waiting for transfers between devices, from_root(): return lax.psum(jnp.where(mine, x, jnp.zeros_like(x)), axis)  86.3 us
    all_gather x11, blocking collectives, one_step(): projected = add_outputs(lax.all_gather(attended, 'tp', axis=1, tiled=True))  78.7 us
    psum x11, blocking collectives, one_step(): mean_sq = lax.psum(partial_sq, 'tp') / MODEL_WIDTH  66.2 us
    all_gather x11, waiting for transfers between devices, one_step(): lax.all_gather(normed, 'tp', axis=1, tiled=True)  61.4 us
    dot_general x11, matrix products, add_columns(): jnp.dot(block_cols, w_keyval, preferred_element_type=jnp.float32)  58.8 us
    all_to_all x11, waiting for transfers between devices, send_pages(): lax.all_to_all(outgoing, 'tp', split_axis=0, concat_axis=0, tiled=True)  47.7 us
  transfers between devices with their start and end apart: 45, of which 34 were waited for; matrix products, arithmetic and copies ran while one was open for 10% of the time, Pallas kernels for 0%

commit v1 on v0

--- a/solution.py
+++ b/solution.py
@@ -8,8 +8,7 @@
 MODEL_WIDTH = 8192
 HEAD_SIZE = 128
 KEY_VALUE_HEADS = 8
-MB_TOK = 64
-MICRO_BATCHES = 8
+MICRO_BATCHES = 4
 PAGE_TOKENS = 4
 
 
@@ -31,61 +30,22 @@
     return lax.psum(jnp.where(mine, x, jnp.zeros_like(x)), axis)
 
 
-def send_pages(kv_own, page_rows, micro_idx, is_live, kv_cache, first_head, tensor_parallel_width):
-    row_count = kv_own.shape[0]
-    kv_cols = kv_own.shape[1]
-    head_width = kv_cache.shape[2]
-    cache_page_count = kv_cache.shape[0]
-    held_heads = max(1, kv_cols // head_width)
-    unit_cols = kv_cols // held_heads
-    blocks = row_count // PAGE_TOKENS
-    paged_rows = (
-        kv_own.reshape(blocks, PAGE_TOKENS, held_heads, unit_cols)
-        .transpose(2, 0, 1, 3)
-        .reshape(held_heads * blocks, PAGE_TOKENS * unit_cols)
+def own_pages(kv_buffer, page_rows, tp_rank, tensor_parallel_width, cache_page_count):
+    row_total = kv_buffer.shape[0]
+    blocks = row_total // PAGE_TOKENS
+    copies = max(1, tensor_parallel_width // KEY_VALUE_HEADS)
+    gathered = lax.all_gather(kv_buffer, "tp", axis=0, tiled=False)[::copies]
+    head_width = 2 * HEAD_SIZE
+    held = kv_buffer.shape[1] // head_width
+    pages = (
+        gathered.reshape(KEY_VALUE_HEADS // held, blocks, PAGE_TOKENS, held, head_width)
+        .transpose(0, 3, 1, 2, 4)
+        .reshape(KEY_VALUE_HEADS * blocks, PAGE_TOKENS * head_width)
     )
-    target_pages = lax.dynamic_slice(
-        page_rows, (first_head, micro_idx * blocks), (held_heads, blocks)
-    ).reshape(-1)
-    device = target_pages // cache_page_count
-    cache_page_index = target_pages % cache_page_count
-    page_count = held_heads * blocks
-    capacity = 2 * page_count // tensor_parallel_width
-    onehot = (
-        device[:, None] == jnp.arange(tensor_parallel_width, dtype=jnp.int32)[None, :]
-    ).astype(jnp.int32)
-    earlier = jnp.cumsum(onehot, axis=0) - onehot
-    arrival = jnp.sum(earlier * onehot, axis=1)
-    position = device * capacity + arrival
-    outgoing = (
-        jnp.zeros((tensor_parallel_width * capacity, PAGE_TOKENS * unit_cols), jnp.bfloat16)
-        .at[position]
-        .set(paged_rows)
-    )
-    labels = (
-        jnp.full((tensor_parallel_width * capacity,), cache_page_count, jnp.int32)
-        .at[position]
-        .set(jnp.where(is_live, cache_page_index, cache_page_count))
-    )
-    incoming, landing = (
-        lax.all_to_all(outgoing, "tp", split_axis=0, concat_axis=0, tiled=True),
-        lax.all_to_all(labels, "tp", split_axis=0, concat_axis=0, tiled=True),
-    )
-    offsets = jnp.arange(tensor_parallel_width, dtype=jnp.int32) * kv_cols % head_width
-    lane_ids = jnp.arange(head_width, dtype=jnp.int32)
-    within = jnp.arange(unit_cols, dtype=jnp.int32)
-    placer = (lane_ids[None, None, :] == offsets[:, None, None] + within[None, :, None]).astype(
-        jnp.bfloat16
-    )
-    spread = jnp.einsum(
-        "snw,swv->snv",
-        incoming.reshape(tensor_parallel_width, capacity * PAGE_TOKENS, unit_cols),
-        placer,
-        preferred_element_type=jnp.float32,
-    ).astype(jnp.bfloat16)
-    return kv_cache.at[landing].add(
-        spread.reshape(tensor_parallel_width * capacity, PAGE_TOKENS, head_width), mode="drop"
-    )
+    slots = tp_rank * cache_page_count + jnp.arange(cache_page_count, dtype=jnp.int32)
+    onehot = (page_rows.reshape(-1)[None, :] == slots[:, None]).astype(jnp.bfloat16)
+    picked = jnp.dot(onehot, pages, preferred_element_type=jnp.float32).astype(jnp.bfloat16)
+    return picked.reshape(cache_page_count, PAGE_TOKENS, head_width)
 
 
 def body(tokens, gain, q_weight, kv_weight, out_weight, page_table, segment_ids):
@@ -99,13 +59,12 @@
     page_rows = page_table[0]
     local_width = tokens.shape[1]
     row_total = tokens.shape[0]
-    row_count = MB_TOK
+    row_count = row_total // MICRO_BATCHES
     head_dim = HEAD_SIZE
     kv_cols = w_keyval.shape[1]
     held_heads = max(1, kv_cols // (2 * head_dim))
     q_heads = w_query.shape[1] // head_dim
     per_kv = q_heads // held_heads
-    first_head = tp_rank * kv_cols // (2 * head_dim)
     cache_page_count = KEY_VALUE_HEADS * (row_total // PAGE_TOKENS) // tensor_parallel_width
     score_scale = 1.0 / math.sqrt(head_dim)
     step_count = MICRO_BATCHES + pp_size - 1
@@ -121,7 +80,7 @@
         return jnp.dot(block_cols, w_output, preferred_element_type=jnp.float32)
 
     def one_step(step_idx, state_tuple):
-        received, kv_buffer, kv_cache, collected = state_tuple
+        received, kv_buffer, collected = state_tuple
         micro_raw = step_idx - section_idx
         is_live = (micro_raw >= 0) & (micro_raw < MICRO_BATCHES)
         micro_idx = jnp.clip(micro_raw, 0, MICRO_BATCHES - 1)
@@ -147,9 +106,6 @@
             )
         else:
             head_pair = kv_own
-        kv_cache = send_pages(
-            kv_own, page_rows, micro_idx, is_live, kv_cache, first_head, tensor_parallel_width
-        )
         refreshed = lax.dynamic_update_slice_in_dim(kv_buffer, head_pair, row_start, 0)
         kv_buffer = jnp.where(is_live, refreshed, kv_buffer)
         kv_view = kv_buffer.reshape(row_total, held_heads, 2, head_dim)
@@ -181,19 +137,21 @@
         placed = lax.dynamic_update_slice_in_dim(collected, produced, row_start, 0)
         collected = jnp.where(is_live & (section_idx == pp_size - 1), placed, collected)
         handed = shifted(produced, "pp", 1)
-        return (handed, kv_buffer, kv_cache, collected)
+        return (handed, kv_buffer, collected)
 
     initial = (
         jnp.zeros((row_count, local_width), jnp.bfloat16),
         jnp.zeros((row_total, held_heads * 2 * head_dim), jnp.bfloat16),
-        jnp.zeros((cache_page_count, PAGE_TOKENS, 2 * head_dim), jnp.bfloat16),
         jnp.zeros((row_total, local_width), jnp.bfloat16),
     )
     finished = lax.fori_loop(0, step_count, one_step, initial)
-    whole_final = from_root(finished[3], "pp", pp_size - 1)
+    whole_final = from_root(finished[2], "pp", pp_size - 1)
     share_rows = row_total // pp_size
     hidden = lax.dynamic_slice_in_dim(whole_final, section_idx * share_rows, share_rows, 0)
-    return (hidden, finished[2][None])
+    kv_cache = own_pages(
+        finished[1], page_rows, tp_rank, tensor_parallel_width, cache_page_count
+    )
+    return (hidden, kv_cache[None])
 
 
 def solution(mesh):

time: 932 us -> 764 us (0.82)
  waiting for transfers between devices: 231 us -> 441 us
  blocking collectives: 145 us -> 44 us
  matrix products: 285 us -> 192 us
  starting transfers between devices: 109 us -> 29.9 us
  local copies, waits for them, and re-layouts: 69.7 us -> 15.4 us
  other arithmetic: 70.3 us -> 24.3 us
    all_gather x0 -> x8, waiting for transfers between devices: none -> 118 us  [the longest x7 118 us: one_step(): projected = add_outputs(lax.all_gather(attended, 'tp', axis=1, tiled=True))]
    all_gather x11 -> x7, waiting for transfers between devices: 61.4 us -> 160 us  [one_step(): lax.all_gather(normed, 'tp', axis=1, tiled=True)]
    all_to_all x22 -> x0, waiting for transfers between devices: 82.8 us -> none  [the longest x11 47.7 us: send_pages(): lax.all_to_all(outgoing, 'tp', split_axis=0, concat_axis=0, tiled=True)]
    all_gather x11 -> x0, blocking collectives: 78.7 us -> none  [one_step(): projected = add_outputs(lax.all_gather(attended, 'tp', axis=1, tiled=True))]
    ppermute x11 -> x7, waiting for transfers between devices: 0.03 us -> 73.8 us  [shifted(): return lax.ppermute(x, axis, pairs)]
    all_to_all x22 -> x0, starting transfers between devices: 72 us -> none  [the longest x11 36.6 us: send_pages(): lax.all_to_all(outgoing, 'tp', split_axis=0, concat_axis=0, tiled=True)]
    dot_general x11 -> x7, matrix products: 96.7 us -> 56.7 us  [add_columns(): jnp.dot(block_cols, w_query, preferred_element_type=jnp.float32)]
    dot_general x11 -> x7, matrix products: 105 us -> 65.2 us  [add_outputs(): return jnp.dot(block_cols, w_output, preferred_element_type=jnp.float32)]
  transfers between devices with their start and end apart: 45 -> 23, of which waited for: 34 -> 22; matrix products, arithmetic and copies ran while one was open for 10% -> 1% of each run, Pallas kernels for 0% -> 0%
where the time goes in v1:
time: 764 us; the launch traced here: 762 us
  waiting for transfers between devices  441 us (58%)
  matrix products  192 us (25%)
  blocking collectives  44 us (6%)
  starting transfers between devices  29.9 us (4%)
  other arithmetic  24.3 us (3%)
  local copies, waits for them, and re-layouts  15.4 us (2%)
  between operations  15.3 us (2%)
    all_gather x7, waiting for transfers between devices, one_step(): lax.all_gather(normed, 'tp', axis=1, tiled=True)  160 us
    all_gather x7, waiting for transfers between devices, one_step(): projected = add_outputs(lax.all_gather(attended, 'tp', axis=1, tiled=True))  118 us
    psum x1, waiting for transfers between devices, from_root(): return lax.psum(jnp.where(mine, x, jnp.zeros_like(x)), axis)  88.3 us
    ppermute x7, waiting for transfers between devices, shifted(): return lax.ppermute(x, axis, pairs)  73.8 us
    dot_general x7, matrix products, add_outputs(): return jnp.dot(block_cols, w_output, preferred_element_type=jnp.float32)  65.2 us
    dot_general x7, matrix products, add_columns(): jnp.dot(block_cols, w_query, preferred_element_type=jnp.float32)  56.7 us
    psum x7, blocking collectives, one_step(): mean_sq = lax.psum(partial_sq, 'tp') / MODEL_WIDTH  44 us
    dot_general x7, matrix products, add_columns(): jnp.dot(block_cols, w_keyval, preferred_element_type=jnp.float32)  37.6 us
  transfers between devices with their start and end apart: 23, of which 22 were waited for; matrix products, arithmetic and copies ran while one was open for 1% of the time, Pallas kernels for 0%

profile of v1, /device:TPU:0, one launch (start us, length us, event | category | flops | bytes accessed | tf_op | source)
XLA Modules:
  0.0 761.9 jit_solution(6642382139610651673)
XLA Ops:
  10.5 645.9 %while.19 = (s32[]{:T(128)}, bf16[128,2048]{1,0:T(8,128)(2,1)}, bf16[512,512]{1,0:T(8,128)(2,1)S(1)}, bf16[512,2048]{1,0:T(8,128)(2,1)}, pred[]{:T(512)}, /*inde...) while((s32[]{:T(128)}, bf16[128,2048]{1,0:T(8,128)(2,1)}, ...), condition=%wide.region_5.6_spmd.clone, body=%wide.region_0.5_spmd.clone.sunk | while | flops 5779821056 | bytes 81760224 | solution.py:147
  12.0 8.4 %psum.22 = f32[128,1]{0,1:T(1,128)S(1)} all-reduce(f32[128,1]{0,1:T(1,128)S(1)} %bitcast.102), channel_id=1, replica_groups=mesh['grp'=2,'tp'=4,'pp'=4] {'tp'}, use_global_device_ids=true, to_apply=%region_2.2 | all-reduce | flops 128 | bytes 1024 | tf_op jit(solution)/shard_map/while/body/eval_jaxpr/psum | solution.py:92
  22.6 22.0 %all-gather.7.cloned.1.call-done = bf16[128,8192]{1,0:T(8,128)(2,1)} async-done(((bf16[128,2048]{1,0:T(8,128)(2,1)}), bf16[128,8192]{1,0:T(8,128)(2,1)}) %all-gather.7.cloned.1.call-update) | async-done | bytes 2097168 | tf_op jit(solution)/shard_map/while/body/eval_jaxpr/all_gather | solution.py:96
  44.6 5.4 fusion.69
  50.2 8.1 %convolution_convert_fusion.6 = bf16[128,1024]{1,0:T(8,128)(2,1)S(1)} fusion(bf16[128,8192]{1,0:T(8,128)(2,1)S(1)} %copy-done, bf16[8192,1024]{1,0:T(8,128)(2,1)} %get-tuple-element.466), kind=kOutput, calls=%fused_computation.11.clone.1 | convolution fusion | flops 2147614720 | bytes 19136512 | tf_op jit(solution)/shard_map/while/body/eval_jaxpr/dot_general | solution.py:75
  60.2 2.7 convolution_convert_fusion.7
  63.0 16.8 %all-gather.9.cloned.1.call-done = bf16[128,4096]{0,1:T(8,128)(2,1)} async-done(((bf16[128,1024]{0,1:T(8,128)(2,1)}), bf16[128,4096]{0,1:T(8,128)(2,1)}) %all-gather.9.cloned.1.call-update) | async-done | bytes 1048592 | tf_op jit(solution)/shard_map/while/body/eval_jaxpr/all_gather | solution.py:135
  79.8 9.3 %select_dynamic-update-slice_fusion.2 = (bf16[512,2048]{1,0:T(8,128)(2,1)}, bf16[128,2048]{1,0:T(8,128)(2,1)S(1)}) fusion(bf16[512,2048]{1,0:T(8,128)(2,1)} %get-tuple-element.440, s32[]{:T(128)S(6)} %select_n.139, pred[]{:T(512)S(6)} %and.39, bf16[128,4096]{0,1:T(8,128)(2,1)} %all-gather.9.cloned.1.call-done, ...), kind=kOutput, calls=%fused_computation.20.clone.1 | convolution fusion | flops 2148532224 | bytes 19922948 | tf_op jit(solution)/shard_map/while/body/eval_jaxpr/dot_general | solution.py:80
  89.2 4.2 collective-permute-start
  93.6 10.5 %collective-permute-done = bf16[128,2048]{1,0:T(8,128)(2,1)} collective-permute-done((bf16[128,2048]{1,0:T(8,128)(2,1)S(1)}, bf16[128,2048]{1,0:T(8,128)(2,1)}, u32[]{:S(2)}, u32[]{:S(2)}) %collective-permute-start) | collective-permute-done | bytes 524320 | tf_op jit(solution)/shard_map/while/body/eval_jaxpr/ppermute | solution.py:25
  105.6 5.9 psum.22
  113.7 23.0 %all-gather.7.cloned.1.call-done = bf16[128,8192]{1,0:T(8,128)(2,1)} async-done(((bf16[128,2048]{1,0:T(8,128)(2,1)}), bf16[128,8192]{1,0:T(8,128)(2,1)}) %all-gather.7.cloned.1.call-update) | async-done | bytes 2097168 | tf_op jit(solution)/shard_map/while/body/eval_jaxpr/all_gather | solution.py:96
  136.7 5.4 fusion.69
  142.2 8.1 %convolution_convert_fusion.6 = bf16[128,1024]{1,0:T(8,128)(2,1)S(1)} fusion(bf16[128,8192]{1,0:T(8,128)(2,1)S(1)} %copy-done, bf16[8192,1024]{1,0:T(8,128)(2,1)} %get-tuple-element.466), kind=kOutput, calls=%fused_computation.11.clone.1 | convolution fusion | flops 2147614720 | bytes 19136512 | tf_op jit(solution)/shard_map/while/body/eval_jaxpr/dot_general | solution.py:75
  152.3 2.7 convolution_convert_fusion.7
  155.0 16.9 %all-gather.9.cloned.1.call-done = bf16[128,4096]{0,1:T(8,128)(2,1)} async-done(((bf16[128,1024]{0,1:T(8,128)(2,1)}), bf16[128,4096]{0,1:T(8,128)(2,1)}) %all-gather.9.cloned.1.call-update) | async-done | bytes 1048592 | tf_op jit(solution)/shard_map/while/body/eval_jaxpr/all_gather | solution.py:135
  171.9 9.3 %select_dynamic-update-slice_fusion.2 = (bf16[512,2048]{1,0:T(8,128)(2,1)}, bf16[128,2048]{1,0:T(8,128)(2,1)S(1)}) fusion(bf16[512,2048]{1,0:T(8,128)(2,1)} %get-tuple-element.440, s32[]{:T(128)S(6)} %select_n.139, pred[]{:T(512)S(6)} %and.39, bf16[128,4096]{0,1:T(8,128)(2,1)} %all-gather.9.cloned.1.call-done, ...), kind=kOutput, calls=%fused_computation.20.clone.1 | convolution fusion | flops 2148532224 | bytes 19922948 | tf_op jit(solution)/shard_map/while/body/eval_jaxpr/dot_general | solution.py:80
  181.2 4.2 collective-permute-start
  185.6 10.5 %collective-permute-done = bf16[128,2048]{1,0:T(8,128)(2,1)} collective-permute-done((bf16[128,2048]{1,0:T(8,128)(2,1)S(1)}, bf16[128,2048]{1,0:T(8,128)(2,1)}, u32[]{:S(2)}, u32[]{:S(2)}) %collective-permute-start) | collective-permute-done | bytes 524320 | tf_op jit(solution)/shard_map/while/body/eval_jaxpr/ppermute | solution.py:25
  197.7 5.9 psum.22
  205.8 23.0 %all-gather.7.cloned.1.call-done = bf16[128,8192]{1,0:T(8,128)(2,1)} async-done(((bf16[128,2048]{1,0:T(8,128)(2,1)}), bf16[128,8192]{1,0:T(8,128)(2,1)}) %all-gather.7.cloned.1.call-update) | async-done | bytes 2097168 | tf_op jit(solution)/shard_map/while/body/eval_jaxpr/all_gather | solution.py:96
  228.8 5.4 fusion.69
  234.3 8.1 %convolution_convert_fusion.6 = bf16[128,1024]{1,0:T(8,128)(2,1)S(1)} fusion(bf16[128,8192]{1,0:T(8,128)(2,1)S(1)} %copy-done, bf16[8192,1024]{1,0:T(8,128)(2,1)} %get-tuple-element.466), kind=kOutput, calls=%fused_computation.11.clone.1 | convolution fusion | flops 2147614720 | bytes 19136512 | tf_op jit(solution)/shard_map/while/body/eval_jaxpr/dot_general | solution.py:75
  247.1 16.9 %all-gather.9.cloned.1.call-done = bf16[128,4096]{0,1:T(8,128)(2,1)} async-done(((bf16[128,1024]{0,1:T(8,128)(2,1)}), bf16[128,4096]{0,1:T(8,128)(2,1)}) %all-gather.9.cloned.1.call-update) | async-done | bytes 1048592 | tf_op jit(solution)/shard_map/while/body/eval_jaxpr/all_gather | solution.py:135
  263.9 9.3 %select_dynamic-update-slice_fusion.2 = (bf16[512,2048]{1,0:T(8,128)(2,1)}, bf16[128,2048]{1,0:T(8,128)(2,1)S(1)}) fusion(bf16[512,2048]{1,0:T(8,128)(2,1)} %get-tuple-element.440, s32[]{:T(128)S(6)} %select_n.139, pred[]{:T(512)S(6)} %and.39, bf16[128,4096]{0,1:T(8,128)(2,1)} %all-gather.9.cloned.1.call-done, ...), kind=kOutput, calls=%fused_computation.20.clone.1 | convolution fusion | flops 2148532224 | bytes 19922948 | tf_op jit(solution)/shard_map/while/body/eval_jaxpr/dot_general | solution.py:80
  273.3 4.2 collective-permute-start
  277.7 10.6 %collective-permute-done = bf16[128,2048]{1,0:T(8,128)(2,1)} collective-permute-done((bf16[128,2048]{1,0:T(8,128)(2,1)S(1)}, bf16[128,2048]{1,0:T(8,128)(2,1)}, u32[]{:S(2)}, u32[]{:S(2)}) %collective-permute-start) | collective-permute-done | bytes 524320 | tf_op jit(solution)/shard_map/while/body/eval_jaxpr/ppermute | solution.py:25
  289.7 5.9 psum.22
  297.8 23.0 %all-gather.7.cloned.1.call-done = bf16[128,8192]{1,0:T(8,128)(2,1)} async-done(((bf16[128,2048]{1,0:T(8,128)(2,1)}), bf16[128,8192]{1,0:T(8,128)(2,1)}) %all-gather.7.cloned.1.call-update) | async-done | bytes 2097168 | tf_op jit(solution)/shard_map/while/body/eval_jaxpr/all_gather | solution.py:96
  320.8 5.4 fusion.69
  326.3 8.1 %convolution_convert_fusion.6 = bf16[128,1024]{1,0:T(8,128)(2,1)S(1)} fusion(bf16[128,8192]{1,0:T(8,128)(2,1)S(1)} %copy-done, bf16[8192,1024]{1,0:T(8,128)(2,1)} %get-tuple-element.466), kind=kOutput, calls=%fused_computation.11.clone.1 | convolution fusion | flops 2147614720 | bytes 19136512 | tf_op jit(solution)/shard_map/while/body/eval_jaxpr/dot_general | solution.py:75
  336.4 2.7 convolution_convert_fusion.7
  339.2 16.9 %all-gather.9.cloned.1.call-done = bf16[128,4096]{0,1:T(8,128)(2,1)} async-done(((bf16[128,1024]{0,1:T(8,128)(2,1)}), bf16[128,4096]{0,1:T(8,128)(2,1)}) %all-gather.9.cloned.1.call-update) | async-done | bytes 1048592 | tf_op jit(solution)/shard_map/while/body/eval_jaxpr/all_gather | solution.py:135
  356.0 9.3 %select_dynamic-update-slice_fusion.2 = (bf16[512,2048]{1,0:T(8,128)(2,1)}, bf16[128,2048]{1,0:T(8,128)(2,1)S(1)}) fusion(bf16[512,2048]{1,0:T(8,128)(2,1)} %get-tuple-element.440, s32[]{:T(128)S(6)} %select_n.139, pred[]{:T(512)S(6)} %and.39, bf16[128,4096]{0,1:T(8,128)(2,1)} %all-gather.9.cloned.1.call-done, ...), kind=kOutput, calls=%fused_computation.20.clone.1 | convolution fusion | flops 2148532224 | bytes 19922948 | tf_op jit(solution)/shard_map/while/body/eval_jaxpr/dot_general | solution.py:80
  365.3 4.2 collective-permute-start
  369.7 10.5 %collective-permute-done = bf16[128,2048]{1,0:T(8,128)(2,1)} collective-permute-done((bf16[128,2048]{1,0:T(8,128)(2,1)S(1)}, bf16[128,2048]{1,0:T(8,128)(2,1)}, u32[]{:S(2)}, u32[]{:S(2)}) %collective-permute-start) | collective-permute-done | bytes 524320 | tf_op jit(solution)/shard_map/while/body/eval_jaxpr/ppermute | solution.py:25
  381.8 5.9 psum.22
  389.9 23.0 %all-gather.7.cloned.1.call-done = bf16[128,8192]{1,0:T(8,128)(2,1)} async-done(((bf16[128,2048]{1,0:T(8,128)(2,1)}), bf16[128,8192]{1,0:T(8,128)(2,1)}) %all-gather.7.cloned.1.call-update) | async-done | bytes 2097168 | tf_op jit(solution)/shard_map/while/body/eval_jaxpr/all_gather | solution.py:96
  412.9 5.4 fusion.69
  418.4 8.1 %convolution_convert_fusion.6 = bf16[128,1024]{1,0:T(8,128)(2,1)S(1)} fusion(bf16[128,8192]{1,0:T(8,128)(2,1)S(1)} %copy-done, bf16[8192,1024]{1,0:T(8,128)(2,1)} %get-tuple-element.466), kind=kOutput, calls=%fused_computation.11.clone.1 | convolution fusion | flops 2147614720 | bytes 19136512 | tf_op jit(solution)/shard_map/while/body/eval_jaxpr/dot_general | solution.py:75
  428.5 2.7 convolution_convert_fusion.7
  431.2 16.9 %all-gather.9.cloned.1.call-done = bf16[128,4096]{0,1:T(8,128)(2,1)} async-done(((bf16[128,1024]{0,1:T(8,128)(2,1)}), bf16[128,4096]{0,1:T(8,128)(2,1)}) %all-gather.9.cloned.1.call-update) | async-done | bytes 1048592 | tf_op jit(solution)/shard_map/while/body/eval_jaxpr/all_gather | solution.py:135
  448.1 9.3 %select_dynamic-update-slice_fusion.2 = (bf16[512,2048]{1,0:T(8,128)(2,1)}, bf16[128,2048]{1,0:T(8,128)(2,1)S(1)}) fusion(bf16[512,2048]{1,0:T(8,128)(2,1)} %get-tuple-element.440, s32[]{:T(128)S(6)} %select_n.139, pred[]{:T(512)S(6)} %and.39, bf16[128,4096]{0,1:T(8,128)(2,1)} %all-gather.9.cloned.1.call-done, ...), kind=kOutput, calls=%fused_computation.20.clone.1 | convolution fusion | flops 2148532224 | bytes 19922948 | tf_op jit(solution)/shard_map/while/body/eval_jaxpr/dot_general | solution.py:80
  457.4 4.2 collective-permute-start
  461.8 10.5 %collective-permute-done = bf16[128,2048]{1,0:T(8,128)(2,1)} collective-permute-done((bf16[128,2048]{1,0:T(8,128)(2,1)S(1)}, bf16[128,2048]{1,0:T(8,128)(2,1)}, u32[]{:S(2)}, u32[]{:S(2)}) %collective-permute-start) | collective-permute-done | bytes 524320 | tf_op jit(solution)/shard_map/while/body/eval_jaxpr/ppermute | solution.py:25
  473.8 5.9 psum.22
  481.9 23.0 %all-gather.7.cloned.1.call-done = bf16[128,8192]{1,0:T(8,128)(2,1)} async-done(((bf16[128,2048]{1,0:T(8,128)(2,1)}), bf16[128,8192]{1,0:T(8,128)(2,1)}) %all-gather.7.cloned.1.call-update) | async-done | bytes 2097168 | tf_op jit(solution)/shard_map/while/body/eval_jaxpr/all_gather | solution.py:96
  504.9 5.4 fusion.69
  510.4 8.1 %convolution_convert_fusion.6 = bf16[128,1024]{1,0:T(8,128)(2,1)S(1)} fusion(bf16[128,8192]{1,0:T(8,128)(2,1)S(1)} %copy-done, bf16[8192,1024]{1,0:T(8,128)(2,1)} %get-tuple-element.466), kind=kOutput, calls=%fused_computation.11.clone.1 | convolution fusion | flops 2147614720 | bytes 19136512 | tf_op jit(solution)/shard_map/while/body/eval_jaxpr/dot_general | solution.py:75
  520.5 2.7 convolution_convert_fusion.7
  523.3 16.8 %all-gather.9.cloned.1.call-done = bf16[128,4096]{0,1:T(8,128)(2,1)} async-done(((bf16[128,1024]{0,1:T(8,128)(2,1)}), bf16[128,4096]{0,1:T(8,128)(2,1)}) %all-gather.9.cloned.1.call-update) | async-done | bytes 1048592 | tf_op jit(solution)/shard_map/while/body/eval_jaxpr/all_gather | solution.py:135
  540.1 9.3 %select_dynamic-update-slice_fusion.2 = (bf16[512,2048]{1,0:T(8,128)(2,1)}, bf16[128,2048]{1,0:T(8,128)(2,1)S(1)}) fusion(bf16[512,2048]{1,0:T(8,128)(2,1)} %get-tuple-element.440, s32[]{:T(128)S(6)} %select_n.139, pred[]{:T(512)S(6)} %and.39, bf16[128,4096]{0,1:T(8,128)(2,1)} %all-gather.9.cloned.1.call-done, ...), kind=kOutput, calls=%fused_computation.20.clone.1 | convolution fusion | flops 2148532224 | bytes 19922948 | tf_op jit(solution)/shard_map/while/body/eval_jaxpr/dot_general | solution.py:80
  549.4 4.2 collective-permute-start
  553.8 10.5 %collective-permute-done = bf16[128,2048]{1,0:T(8,128)(2,1)} collective-permute-done((bf16[128,2048]{1,0:T(8,128)(2,1)S(1)}, bf16[128,2048]{1,0:T(8,128)(2,1)}, u32[]{:S(2)}, u32[]{:S(2)}) %collective-permute-start) | collective-permute-done | bytes 524320 | tf_op jit(solution)/shard_map/while/body/eval_jaxpr/ppermute | solution.py:25
  565.9 5.9 psum.22
  574.0 23.0 %all-gather.7.cloned.1.call-done = bf16[128,8192]{1,0:T(8,128)(2,1)} async-done(((bf16[128,2048]{1,0:T(8,128)(2,1)}), bf16[128,8192]{1,0:T(8,128)(2,1)}) %all-gather.7.cloned.1.call-update) | async-done | bytes 2097168 | tf_op jit(solution)/shard_map/while/body/eval_jaxpr/all_gather | solution.py:96
  597.0 5.4 fusion.69
  602.5 8.1 %convolution_convert_fusion.6 = bf16[128,1024]{1,0:T(8,128)(2,1)S(1)} fusion(bf16[128,8192]{1,0:T(8,128)(2,1)S(1)} %copy-done, bf16[8192,1024]{1,0:T(8,128)(2,1)} %get-tuple-element.466), kind=kOutput, calls=%fused_computation.11.clone.1 | convolution fusion | flops 2147614720 | bytes 19136512 | tf_op jit(solution)/shard_map/while/body/eval_jaxpr/dot_general | solution.py:75
  612.6 2.7 convolution_convert_fusion.7
  615.3 16.9 %all-gather.9.cloned.1.call-done = bf16[128,4096]{0,1:T(8,128)(2,1)} async-done(((bf16[128,1024]{0,1:T(8,128)(2,1)}), bf16[128,4096]{0,1:T(8,128)(2,1)}) %all-gather.9.cloned.1.call-update) | async-done | bytes 1048592 | tf_op jit(solution)/shard_map/while/body/eval_jaxpr/all_gather | solution.py:135
  632.2 9.3 %select_dynamic-update-slice_fusion.2 = (bf16[512,2048]{1,0:T(8,128)(2,1)}, bf16[128,2048]{1,0:T(8,128)(2,1)S(1)}) fusion(bf16[512,2048]{1,0:T(8,128)(2,1)} %get-tuple-element.440, s32[]{:T(128)S(6)} %select_n.139, pred[]{:T(512)S(6)} %and.39, bf16[128,4096]{0,1:T(8,128)(2,1)} %all-gather.9.cloned.1.call-done, ...), kind=kOutput, calls=%fused_computation.20.clone.1 | convolution fusion | flops 2148532224 | bytes 19922948 | tf_op jit(solution)/shard_map/while/body/eval_jaxpr/dot_general | solution.py:80
  641.5 4.2 collective-permute-start
  645.9 10.6 %collective-permute-done = bf16[128,2048]{1,0:T(8,128)(2,1)} collective-permute-done((bf16[128,2048]{1,0:T(8,128)(2,1)S(1)}, bf16[128,2048]{1,0:T(8,128)(2,1)}, u32[]{:S(2)}, u32[]{:S(2)}) %collective-permute-start) | collective-permute-done | bytes 524320 | tf_op jit(solution)/shard_map/while/body/eval_jaxpr/ppermute | solution.py:25
  658.6 88.3 %all-reduce.2.cloned.1.call-done = bf16[512,2048]{1,0:T(8,128)(2,1)} async-done(((bf16[512,2048]{1,0:T(8,128)(2,1)}), bf16[512,2048]{1,0:T(8,128)(2,1)}) %all-reduce.2.cloned.1.call-update) | async-done | bytes 2097168 | tf_op jit(solution)/shard_map/psum | solution.py:30
  (172 shorter events, 56.5 us)
Async XLA Ops:
  8.0 2.5 copy-start.3
  8.0 2.5 copy-start.4
  10.5 11.2 %copy-start.1 = (bf16[512,512]{1,0:T(8,128)(2,1)}, bf16[512,512]{1,0:T(8,128)(2,1)S(1)}, u32[]{:S(2)}) copy-start(bf16[512,512]{1,0:T(8,128)(2,1)S(1)} %get-tuple-element.439) | copy-start | bytes 1572868 | tf_op jit(solution)/shard_map/while
  10.5 34.1 %all-gather.7.cloned.1.call-start = ((), (), s32[]{:S(2)}) async-start(), calls=%async_computation.2 | async-start | bytes 2621440 | tf_op jit(solution)/shard_map/while/body/eval_jaxpr/all_gather | solution.py:96
  21.5 58.4 %all-gather.9.cloned.1.call-start = ((), (), s32[]{:S(2)}) async-start(), calls=%async_computation.3 | async-start | bytes 1310720 | tf_op jit(solution)/shard_map/while/body/eval_jaxpr/all_gather | solution.py:135
  44.6 5.5 copy-start
  89.2 14.9 %collective-permute-start = (bf16[128,2048]{1,0:T(8,128)(2,1)S(1)}, bf16[128,2048]{1,0:T(8,128)(2,1)}, u32[]{:S(2)}, u32[]{:S(2)}) collective-permute-start(bf16[128,2048]{1,0:T(8,128)(2,1)S(1)} %get-tuple-element.416), channel_id=1, source_target_pairs={{0,1},{1,2},{2,3},{4,5},{5,6},{6,7},{8,9},{9,10},{10,11},{12,13},{... | collective-permute-start | bytes 1572872 | tf_op jit(solution)/shard_map/while/body/eval_jaxpr/ppermute | solution.py:25
  104.1 8.7 %copy-start.1 = (bf16[512,512]{1,0:T(8,128)(2,1)}, bf16[512,512]{1,0:T(8,128)(2,1)S(1)}, u32[]{:S(2)}) copy-start(bf16[512,512]{1,0:T(8,128)(2,1)S(1)} %get-tuple-element.439) | copy-start | bytes 1572868 | tf_op jit(solution)/shard_map/while
  104.1 32.6 %all-gather.7.cloned.1.call-start = ((), (), s32[]{:S(2)}) async-start(), calls=%async_computation.2 | async-start | bytes 2621440 | tf_op jit(solution)/shard_map/while/body/eval_jaxpr/all_gather | solution.py:96
  112.6 59.3 %all-gather.9.cloned.1.call-start = ((), (), s32[]{:S(2)}) async-start(), calls=%async_computation.3 | async-start | bytes 1310720 | tf_op jit(solution)/shard_map/while/body/eval_jaxpr/all_gather | solution.py:135
  136.7 5.5 copy-start
  181.2 14.9 %collective-permute-start = (bf16[128,2048]{1,0:T(8,128)(2,1)S(1)}, bf16[128,2048]{1,0:T(8,128)(2,1)}, u32[]{:S(2)}, u32[]{:S(2)}) collective-permute-start(bf16[128,2048]{1,0:T(8,128)(2,1)S(1)} %get-tuple-element.416), channel_id=1, source_target_pairs={{0,1},{1,2},{2,3},{4,5},{5,6},{6,7},{8,9},{9,10},{10,11},{12,13},{... | collective-permute-start | bytes 1572872 | tf_op jit(solution)/shard_map/while/body/eval_jaxpr/ppermute | solution.py:25
  196.2 8.8 %copy-start.1 = (bf16[512,512]{1,0:T(8,128)(2,1)}, bf16[512,512]{1,0:T(8,128)(2,1)S(1)}, u32[]{:S(2)}) copy-start(bf16[512,512]{1,0:T(8,128)(2,1)S(1)} %get-tuple-element.439) | copy-start | bytes 1572868 | tf_op jit(solution)/shard_map/while
  196.2 32.6 %all-gather.7.cloned.1.call-start = ((), (), s32[]{:S(2)}) async-start(), calls=%async_computation.2 | async-start | bytes 2621440 | tf_op jit(solution)/shard_map/while/body/eval_jaxpr/all_gather | solution.py:96
  204.6 59.3 %all-gather.9.cloned.1.call-start = ((), (), s32[]{:S(2)}) async-start(), calls=%async_computation.3 | async-start | bytes 1310720 | tf_op jit(solution)/shard_map/while/body/eval_jaxpr/all_gather | solution.py:135
  228.8 5.5 copy-start
  273.3 14.9 %collective-permute-start = (bf16[128,2048]{1,0:T(8,128)(2,1)S(1)}, bf16[128,2048]{1,0:T(8,128)(2,1)}, u32[]{:S(2)}, u32[]{:S(2)}) collective-permute-start(bf16[128,2048]{1,0:T(8,128)(2,1)S(1)} %get-tuple-element.416), channel_id=1, source_target_pairs={{0,1},{1,2},{2,3},{4,5},{5,6},{6,7},{8,9},{9,10},{10,11},{12,13},{... | collective-permute-start | bytes 1572872 | tf_op jit(solution)/shard_map/while/body/eval_jaxpr/ppermute | solution.py:25
  288.2 8.8 %copy-start.1 = (bf16[512,512]{1,0:T(8,128)(2,1)}, bf16[512,512]{1,0:T(8,128)(2,1)S(1)}, u32[]{:S(2)}) copy-start(bf16[512,512]{1,0:T(8,128)(2,1)S(1)} %get-tuple-element.439) | copy-start | bytes 1572868 | tf_op jit(solution)/shard_map/while
  288.2 32.6 %all-gather.7.cloned.1.call-start = ((), (), s32[]{:S(2)}) async-start(), calls=%async_computation.2 | async-start | bytes 2621440 | tf_op jit(solution)/shard_map/while/body/eval_jaxpr/all_gather | solution.py:96
  296.7 59.3 %all-gather.9.cloned.1.call-start = ((), (), s32[]{:S(2)}) async-start(), calls=%async_computation.3 | async-start | bytes 1310720 | tf_op jit(solution)/shard_map/while/body/eval_jaxpr/all_gather | solution.py:135
  320.8 5.5 copy-start
  365.3 15.0 %collective-permute-start = (bf16[128,2048]{1,0:T(8,128)(2,1)S(1)}, bf16[128,2048]{1,0:T(8,128)(2,1)}, u32[]{:S(2)}, u32[]{:S(2)}) collective-permute-start(bf16[128,2048]{1,0:T(8,128)(2,1)S(1)} %get-tuple-element.416), channel_id=1, source_target_pairs={{0,1},{1,2},{2,3},{4,5},{5,6},{6,7},{8,9},{9,10},{10,11},{12,13},{... | collective-permute-start | bytes 1572872 | tf_op jit(solution)/shard_map/while/body/eval_jaxpr/ppermute | solution.py:25
  380.3 8.7 %copy-start.1 = (bf16[512,512]{1,0:T(8,128)(2,1)}, bf16[512,512]{1,0:T(8,128)(2,1)S(1)}, u32[]{:S(2)}) copy-start(bf16[512,512]{1,0:T(8,128)(2,1)S(1)} %get-tuple-element.439) | copy-start | bytes 1572868 | tf_op jit(solution)/shard_map/while
  380.3 32.6 %all-gather.7.cloned.1.call-start = ((), (), s32[]{:S(2)}) async-start(), calls=%async_computation.2 | async-start | bytes 2621440 | tf_op jit(solution)/shard_map/while/body/eval_jaxpr/all_gather | solution.py:96
  388.7 59.3 %all-gather.9.cloned.1.call-start = ((), (), s32[]{:S(2)}) async-start(), calls=%async_computation.3 | async-start | bytes 1310720 | tf_op jit(solution)/shard_map/while/body/eval_jaxpr/all_gather | solution.py:135
  412.9 5.5 copy-start
  457.4 14.9 %collective-permute-start = (bf16[128,2048]{1,0:T(8,128)(2,1)S(1)}, bf16[128,2048]{1,0:T(8,128)(2,1)}, u32[]{:S(2)}, u32[]{:S(2)}) collective-permute-start(bf16[128,2048]{1,0:T(8,128)(2,1)S(1)} %get-tuple-element.416), channel_id=1, source_target_pairs={{0,1},{1,2},{2,3},{4,5},{5,6},{6,7},{8,9},{9,10},{10,11},{12,13},{... | collective-permute-start | bytes 1572872 | tf_op jit(solution)/shard_map/while/body/eval_jaxpr/ppermute | solution.py:25
  472.3 8.7 %copy-start.1 = (bf16[512,512]{1,0:T(8,128)(2,1)}, bf16[512,512]{1,0:T(8,128)(2,1)S(1)}, u32[]{:S(2)}) copy-start(bf16[512,512]{1,0:T(8,128)(2,1)S(1)} %get-tuple-element.439) | copy-start | bytes 1572868 | tf_op jit(solution)/shard_map/while
  472.3 32.6 %all-gather.7.cloned.1.call-start = ((), (), s32[]{:S(2)}) async-start(), calls=%async_computation.2 | async-start | bytes 2621440 | tf_op jit(solution)/shard_map/while/body/eval_jaxpr/all_gather | solution.py:96
  480.8 59.3 %all-gather.9.cloned.1.call-start = ((), (), s32[]{:S(2)}) async-start(), calls=%async_computation.3 | async-start | bytes 1310720 | tf_op jit(solution)/shard_map/while/body/eval_jaxpr/all_gather | solution.py:135
  504.9 5.5 copy-start
  549.4 14.9 %collective-permute-start = (bf16[128,2048]{1,0:T(8,128)(2,1)S(1)}, bf16[128,2048]{1,0:T(8,128)(2,1)}, u32[]{:S(2)}, u32[]{:S(2)}) collective-permute-start(bf16[128,2048]{1,0:T(8,128)(2,1)S(1)} %get-tuple-element.416), channel_id=1, source_target_pairs={{0,1},{1,2},{2,3},{4,5},{5,6},{6,7},{8,9},{9,10},{10,11},{12,13},{... | collective-permute-start | bytes 1572872 | tf_op jit(solution)/shard_map/while/body/eval_jaxpr/ppermute | solution.py:25
  564.4 8.7 %copy-start.1 = (bf16[512,512]{1,0:T(8,128)(2,1)}, bf16[512,512]{1,0:T(8,128)(2,1)S(1)}, u32[]{:S(2)}) copy-start(bf16[512,512]{1,0:T(8,128)(2,1)S(1)} %get-tuple-element.439) | copy-start | bytes 1572868 | tf_op jit(solution)/shard_map/while
  564.4 32.6 %all-gather.7.cloned.1.call-start = ((), (), s32[]{:S(2)}) async-start(), calls=%async_computation.2 | async-start | bytes 2621440 | tf_op jit(solution)/shard_map/while/body/eval_jaxpr/all_gather | solution.py:96
  572.8 59.3 %all-gather.9.cloned.1.call-start = ((), (), s32[]{:S(2)}) async-start(), calls=%async_computation.3 | async-start | bytes 1310720 | tf_op jit(solution)/shard_map/while/body/eval_jaxpr/all_gather | solution.py:135
  597.0 5.5 copy-start
  641.5 14.9 %collective-permute-start = (bf16[128,2048]{1,0:T(8,128)(2,1)S(1)}, bf16[128,2048]{1,0:T(8,128)(2,1)}, u32[]{:S(2)}, u32[]{:S(2)}) collective-permute-start(bf16[128,2048]{1,0:T(8,128)(2,1)S(1)} %get-tuple-element.416), channel_id=1, source_target_pairs={{0,1},{1,2},{2,3},{4,5},{5,6},{6,7},{8,9},{9,10},{10,11},{12,13},{... | collective-permute-start | bytes 1572872 | tf_op jit(solution)/shard_map/while/body/eval_jaxpr/ppermute | solution.py:25
  656.4 1.5 copy-start.2
  656.4 90.4 %all-reduce.2.cloned.1.call-start = ((), (), s32[]{:S(2)}) async-start(), calls=%async_computation | async-start | bytes 4194304 | tf_op jit(solution)/shard_map/psum | solution.py:30
  658.0 90.8 %all-gather.5.cloned.1.call-start = ((), (), s32[]{:S(2)}) async-start(), calls=%async_computation.1 | async-start | bytes 2621440 | tf_op jit(solution)/shard_map/all_gather | solution.py:37
  752.1 0.7 copy-start.5
Sparse Core Ops, SparseCore 0:
  21.6 23.0 all-gather.6
  63.1 16.6 all-gather.8
  112.7 23.9 all-gather.6
  155.2 16.6 all-gather.8
  204.8 23.9 all-gather.6
  247.2 16.6 all-gather.8
  296.8 23.9 all-gather.6
  339.3 16.6 all-gather.8
  388.9 23.9 all-gather.6
  431.3 16.6 all-gather.8
  480.9 23.9 all-gather.6
  523.4 16.6 all-gather.8
  573.0 23.9 all-gather.6
  615.4 16.6 all-gather.8
  660.6 25.3 all-gather.4
Sparse Core Ops, SparseCore 1:
  659.3 87.5 all-reduce.1

commit v2 on v1

--- a/solution.py
+++ b/solution.py
@@ -8,7 +8,6 @@
 MODEL_WIDTH = 8192
 HEAD_SIZE = 128
 KEY_VALUE_HEADS = 8
-MICRO_BATCHES = 4
 PAGE_TOKENS = 4
 
 
@@ -23,11 +22,6 @@
     peers = lax.axis_size(axis)
     pairs = [(i, i + by) for i in range(peers) if 0 <= i + by < peers]
     return lax.ppermute(x, axis, pairs)
-
-
-def from_root(x, axis, root):
-    mine = lax.axis_index(axis) == root
-    return lax.psum(jnp.where(mine, x, jnp.zeros_like(x)), axis)
 
 
 def own_pages(kv_buffer, page_rows, tp_rank, tensor_parallel_width, cache_page_count):
@@ -59,7 +53,8 @@
     page_rows = page_table[0]
     local_width = tokens.shape[1]
     row_total = tokens.shape[0]
-    row_count = row_total // MICRO_BATCHES
+    micro_batches = pp_size
+    row_count = row_total // micro_batches
     head_dim = HEAD_SIZE
     kv_cols = w_keyval.shape[1]
     held_heads = max(1, kv_cols // (2 * head_dim))
@@ -67,8 +62,8 @@
     per_kv = q_heads // held_heads
     cache_page_count = KEY_VALUE_HEADS * (row_total // PAGE_TOKENS) // tensor_parallel_width
     score_scale = 1.0 / math.sqrt(head_dim)
-    step_count = MICRO_BATCHES + pp_size - 1
-    key_pos = jnp.arange(row_total, dtype=jnp.int32)
+    step_count = micro_batches + pp_size - 1
+    gain_all = lax.all_gather(gain, "tp", axis=1, tiled=True).astype(jnp.float32)
 
     def add_columns(block_cols):
         return (
@@ -80,20 +75,17 @@
         return jnp.dot(block_cols, w_output, preferred_element_type=jnp.float32)
 
     def one_step(step_idx, state_tuple):
-        received, kv_buffer, collected = state_tuple
+        received, kv_buffer, hidden = state_tuple
         micro_raw = step_idx - section_idx
-        is_live = (micro_raw >= 0) & (micro_raw < MICRO_BATCHES)
-        micro_idx = jnp.clip(micro_raw, 0, MICRO_BATCHES - 1)
+        is_live = (micro_raw >= 0) & (micro_raw < micro_batches)
+        micro_idx = jnp.clip(micro_raw, 0, micro_batches - 1)
         row_start = micro_idx * row_count
         first_rows = lax.dynamic_slice_in_dim(tokens, row_start, row_count, 0)
         current = jnp.where(section_idx == 0, first_rows, received)
-        widened = current.astype(jnp.float32)
-        partial_sq = jnp.sum(widened * widened, axis=1, keepdims=True)
-        mean_sq = lax.psum(partial_sq, "tp") / MODEL_WIDTH
-        normed = (widened * lax.rsqrt(mean_sq + eps_norm) * gain.astype(jnp.float32)).astype(
-            jnp.bfloat16
-        )
-        query_sum, keyval_sum = add_columns(lax.all_gather(normed, "tp", axis=1, tiled=True))
+        whole_rows = lax.all_gather(current, "tp", axis=1, tiled=True).astype(jnp.float32)
+        mean_sq = jnp.sum(whole_rows * whole_rows, axis=1, keepdims=True) / MODEL_WIDTH
+        normed = (whole_rows * lax.rsqrt(mean_sq + eps_norm) * gain_all).astype(jnp.bfloat16)
+        query_sum, keyval_sum = add_columns(normed)
         query_matrix = query_sum.astype(jnp.bfloat16)
         kv_own = keyval_sum.astype(jnp.bfloat16)
         if tensor_parallel_width > KEY_VALUE_HEADS:
@@ -108,7 +100,9 @@
             head_pair = kv_own
         refreshed = lax.dynamic_update_slice_in_dim(kv_buffer, head_pair, row_start, 0)
         kv_buffer = jnp.where(is_live, refreshed, kv_buffer)
-        kv_view = kv_buffer.reshape(row_total, held_heads, 2, head_dim)
+        key_count = row_count * min(step_idx + 1, micro_batches)
+        key_pos = jnp.arange(key_count, dtype=jnp.int32)
+        kv_view = kv_buffer[:key_count].reshape(key_count, held_heads, 2, head_dim)
         grouped_queries = query_matrix.reshape(row_count, held_heads, per_kv, head_dim)
         scores = (
             jnp.einsum(
@@ -122,7 +116,7 @@
         query_pos = row_start + jnp.arange(row_count, dtype=jnp.int32)
         seg_query = lax.dynamic_slice_in_dim(segment_ids, row_start, row_count, 0)
         allowed = (key_pos[None, :] <= query_pos[:, None]) & (
-            segment_ids[None, :] == seg_query[:, None]
+            segment_ids[None, :key_count] == seg_query[:, None]
         )
         scores = jnp.where(allowed[None, None], scores, -1e30)
         row_max = jnp.max(scores, axis=-1, keepdims=True)
@@ -133,21 +127,25 @@
         )
         attended = attended.astype(jnp.bfloat16).reshape(row_count, q_heads * head_dim)
         projected = add_outputs(lax.all_gather(attended, "tp", axis=1, tiled=True))
-        produced = (widened + projected).astype(jnp.bfloat16)
-        placed = lax.dynamic_update_slice_in_dim(collected, produced, row_start, 0)
-        collected = jnp.where(is_live & (section_idx == pp_size - 1), placed, collected)
-        handed = shifted(produced, "pp", 1)
-        return (handed, kv_buffer, collected)
+        produced = (current.astype(jnp.float32) + projected).astype(jnp.bfloat16)
+        done = step_idx - (pp_size - 1)
+        if done >= 0:
+            share = produced
+            if done < pp_size - 1:
+                share = lax.ppermute(produced, "pp", [(pp_size - 1, done)])
+            hidden = jnp.where(section_idx == done, share, hidden)
+        handed = shifted(produced, "pp", 1) if step_idx < step_count - 1 else produced
+        return (handed, kv_buffer, hidden)
 
     initial = (
         jnp.zeros((row_count, local_width), jnp.bfloat16),
         jnp.zeros((row_total, held_heads * 2 * head_dim), jnp.bfloat16),
-        jnp.zeros((row_total, local_width), jnp.bfloat16),
+        jnp.zeros((row_count, local_width), jnp.bfloat16),
     )
-    finished = lax.fori_loop(0, step_count, one_step, initial)
-    whole_final = from_root(finished[2], "pp", pp_size - 1)
-    share_rows = row_total // pp_size
-    hidden = lax.dynamic_slice_in_dim(whole_final, section_idx * share_rows, share_rows, 0)
+    finished = initial
+    for step_idx in range(step_count):
+        finished = one_step(step_idx, finished)
+    hidden = finished[2]
     kv_cache = own_pages(
         finished[1], page_rows, tp_rank, tensor_parallel_width, cache_page_count
     )

time: 764 us -> 648 us (0.85)
  waiting for transfers between devices: 441 us -> 355 us
  blocking collectives: 44 us -> 6.45 us
  local copies, waits for them, and re-layouts: 15.4 us -> 26.5 us
  matrix products: 192 us -> 184 us
    psum x1 -> x0, waiting for transfers between devices: 88.3 us -> none  [from_root(): return lax.psum(jnp.where(mine, x, jnp.zeros_like(x)), axis)]
    psum x7 -> x0, blocking collectives: 44 us -> none  [one_step(): mean_sq = lax.psum(partial_sq, 'tp') / MODEL_WIDTH]
    all_gather x1, waiting for transfers between devices: 0.01 us -> 14.4 us  [own_pages(): gathered = lax.all_gather(kv_buffer, 'tp', axis=0, tiled=False)[::copies]]
    ppermute x7 -> x6, starting transfers between devices: 29.3 us -> 20.9 us  [shifted(): return lax.ppermute(x, axis, pairs)]
    slice x0 -> x12, local copies, waits for them, and re-layouts: none -> 8.35 us  [the longest x6 8.17 us: one_step(): kv_view[:, :, 1]]
    unnamed x9 -> x71, local copies, waits for them, and re-layouts: 0.69 us -> 8.87 us
    ppermute x7 -> x6, waiting for transfers between devices: 73.8 us -> 69.1 us  [shifted(): return lax.ppermute(x, axis, pairs)]
  transfers between devices with their start and end apart: 23 -> 24, of which waited for: 22 -> 21; matrix products, arithmetic and copies ran while one was open for 1% -> 2% of each run, Pallas kernels for 0% -> 0%
where the time goes in v2:
time: 648 us; the launch traced here: 641 us
  waiting for transfers between devices  355 us (55%)
  matrix products  184 us (28%)
  other arithmetic  27.1 us (4%)
  starting transfers between devices  26.9 us (4%)
  local copies, waits for them, and re-layouts  26.5 us (4%)
  between operations  15.4 us (2%)
    all_gather x7, waiting for transfers between devices, one_step(): lax.all_gather(current, 'tp', axis=1, tiled=True).astype(jnp.float32)  157 us
    all_gather x7, waiting for transfers between devices, one_step(): projected = add_outputs(lax.all_gather(attended, 'tp', axis=1, tiled=True))  113 us
    ppermute x6, waiting for transfers between devices, shifted(): return lax.ppermute(x, axis, pairs)  69.1 us
    dot_general x7, matrix products, add_outputs(): return jnp.dot(block_cols, w_output, preferred_element_type=jnp.float32)  59.3 us
    dot_general x7, matrix products, add_columns(): jnp.dot(block_cols, w_query, preferred_element_type=jnp.float32)  57.6 us
    dot_general x7, matrix products, add_columns(): jnp.dot(block_cols, w_keyval, preferred_element_type=jnp.float32)  36 us
    ppermute x6, starting transfers between devices, shifted(): return lax.ppermute(x, axis, pairs)  20.9 us
    dot_general x7, matrix products, one_step(): jnp.einsum('gpqk,kgd->qgpd', weights, kv_view[:, :, 1], preferred_element...  17 us
  transfers between devices with their start and end apart: 24, of which 21 were waited for; matrix products, arithmetic and copies ran while one was open for 2% of the time, Pallas kernels for 0%

profile of v2, /device:TPU:0, one launch (start us, length us, event | category | flops | bytes accessed | tf_op | source)
XLA Modules:
  0.0 640.6 jit_solution(9808062135441615010)
XLA Ops:
  9.3 6.4 %all_gather.52 = bf16[1,8192]{1,0:T(2,128)(2,1)S(1)} all-gather(bf16[1,2048]{1,0:T(2,128)(2,1)} %param.8), channel_id=1, replica_groups=mesh['grp'=2,'tp'=4,'pp'=4] {'tp'}, dimensions={1}, use_global_device_ids=true | all-gather | bytes 20480 | tf_op jit(solution)/shard_map/all_gather | solution.py:66
  17.5 17.9 %all-gather.17.cloned.1.call-done = bf16[128,8192]{1,0:T(8,128)(2,1)} async-done(((bf16[128,2048]{1,0:T(8,128)(2,1)}), bf16[128,8192]{1,0:T(8,128)(2,1)}) %all-gather.17.cloned.1.call-update) | async-done | bytes 2097168 | tf_op jit(solution)/shard_map/all_gather | solution.py:85
  35.4 2.2 fusion.49
  37.7 8.1 %fusion.90 = bf16[128,1024]{1,0:T(8,128)(2,1)S(1)} fusion(bf16[1,8192,1024]{2,1,0:T(8,128)(2,1)} %param.9, bf16[128,8192]{1,0:T(8,128)(2,1)S(1)} %copy-done.9, f32[8192]{0:T(1024)S(1)} %bitcast.384, f32[128]{0:T(128)S(1)} %add_rsqrt_fusion.6), kind=kOutput, calls=%fused_computation.124 | convolution fusion | flops 2151809024 | bytes 19169792 | tf_op jit(solution)/shard_map/dot_general | solution.py:70
  46.1 4.7 fusion.171
  52.6 16.8 %all-gather.19.cloned.1.call-done = bf16[128,4096]{0,1:T(8,128)(2,1)} async-done(((bf16[128,1024]{0,1:T(8,128)(2,1)}), bf16[128,4096]{0,1:T(8,128)(2,1)}) %all-gather.19.cloned.1.call-update) | async-done | bytes 1048592 | tf_op jit(solution)/shard_map/all_gather | solution.py:129
  69.4 8.5 %fusion.73 = bf16[128,2048]{1,0:T(8,128)(2,1)S(1)} fusion(bf16[128,4096]{0,1:T(8,128)(2,1)} %all-gather.19.cloned.1.call-done, bf16[1,4096,2048]{2,1,0:T(8,128)(2,1)} %param.11, bf16[128,2048]{1,0:T(8,128)(2,1)S(1)} %copy-done.2), kind=kOutput, calls=%fused_computation.85 | convolution fusion | flops 2148270080 | bytes 18874368 | tf_op jit(solution)/shard_map/dot_general | solution.py:75
  77.9 3.4 collective-permute-start
  81.3 11.5 %collective-permute-done = bf16[128,2048]{1,0:T(8,128)(2,1)S(1)} collective-permute-done((bf16[128,2048]{1,0:T(8,128)(2,1)S(1)}, bf16[128,2048]{1,0:T(8,128)(2,1)S(1)}, u32[]{:S(2)}, u32[]{:S(2)}) %collective-permute-start) | collective-permute-done | bytes 524320 | tf_op jit(solution)/shard_map/ppermute | solution.py:24
  94.2 23.3 %all-gather.21.cloned.1.call-done = bf16[128,8192]{1,0:T(8,128)(2,1)} async-done(((bf16[128,2048]{1,0:T(8,128)(2,1)}), bf16[128,8192]{1,0:T(8,128)(2,1)}) %all-gather.21.cloned.1.call-update) | async-done | bytes 2097168 | tf_op jit(solution)/shard_map/all_gather | solution.py:85
  117.5 2.2 fusion.52
  119.8 8.3 %fusion.93 = bf16[128,1024]{1,0:T(8,128)(2,1)S(1)} fusion(bf16[1,8192,1024]{2,1,0:T(8,128)(2,1)} %param.9, bf16[128,8192]{1,0:T(8,128)(2,1)S(1)} %copy-done.11, f32[128]{0:T(128)S(1)} %add_rsqrt_fusion.5, f32[8192]{0:T(1024)S(1)} %bitcast.386), kind=kOutput, calls=%fused_computation.125 | convolution fusion | flops 2151809024 | bytes 19169792 | tf_op jit(solution)/shard_map/dot_general | solution.py:70
  128.2 5.3 fusion.165
  137.7 2.7 convolution_convert_fusion.5
  140.5 16.8 %all-gather.23.cloned.1.call-done = bf16[128,4096]{0,1:T(8,128)(2,1)} async-done(((bf16[128,1024]{0,1:T(8,128)(2,1)}), bf16[128,4096]{0,1:T(8,128)(2,1)}) %all-gather.23.cloned.1.call-update) | async-done | bytes 1048592 | tf_op jit(solution)/shard_map/all_gather | solution.py:129
  157.3 8.5 %add_convert_fusion.5 = bf16[128,2048]{1,0:T(8,128)(2,1)S(1)} fusion(bf16[128,2048]{1,0:T(8,128)(2,1)S(1)} %copy-done.5, bf16[128,4096]{0,1:T(8,128)(2,1)} %all-gather.23.cloned.1.call-done, bf16[1,4096,2048]{2,1,0:T(8,128)(2,1)} %param.11), kind=kOutput, calls=%fused_computation.165 | convolution fusion | flops 2148270080 | bytes 18874368 | tf_op jit(solution)/shard_map/dot_general | solution.py:75
  165.8 3.4 collective-permute-start.1
  169.2 11.5 %collective-permute-done.1 = bf16[128,2048]{1,0:T(8,128)(2,1)S(1)} collective-permute-done((bf16[128,2048]{1,0:T(8,128)(2,1)S(1)}, bf16[128,2048]{1,0:T(8,128)(2,1)S(1)}, u32[]{:S(2)}, u32[]{:S(2)}) %collective-permute-start.1) | collective-permute-done | bytes 524320 | tf_op jit(solution)/shard_map/ppermute | solution.py:24
  182.1 23.3 %all-gather.25.cloned.1.call-done = bf16[128,8192]{1,0:T(8,128)(2,1)} async-done(((bf16[128,2048]{1,0:T(8,128)(2,1)}), bf16[128,8192]{1,0:T(8,128)(2,1)}) %all-gather.25.cloned.1.call-update) | async-done | bytes 2097168 | tf_op jit(solution)/shard_map/all_gather | solution.py:85
  205.4 2.2 fusion.55
  207.6 8.2 %fusion.96 = bf16[128,1024]{1,0:T(8,128)(2,1)S(1)} fusion(bf16[1,8192,1024]{2,1,0:T(8,128)(2,1)} %param.9, bf16[128,8192]{1,0:T(8,128)(2,1)S(1)} %copy-done.12, f32[128]{0:T(128)S(1)} %add_rsqrt_fusion.4, f32[8192]{0:T(1024)S(1)} %bitcast.388), kind=kOutput, calls=%fused_computation.126 | convolution fusion | flops 2151809024 | bytes 19169792 | tf_op jit(solution)/shard_map/dot_general | solution.py:70
  216.8 5.3 fusion.159
  224.7 2.9 fusion.326
  227.6 2.5 convolution_convert_fusion.7
  230.2 16.8 %all-gather.27.cloned.1.call-done = bf16[128,4096]{0,1:T(8,128)(2,1)} async-done(((bf16[128,1024]{0,1:T(8,128)(2,1)}), bf16[128,4096]{0,1:T(8,128)(2,1)}) %all-gather.27.cloned.1.call-update) | async-done | bytes 1048592 | tf_op jit(solution)/shard_map/all_gather | solution.py:129
  247.0 8.5 %add_convert_fusion.4 = bf16[128,2048]{1,0:T(8,128)(2,1)S(1)} fusion(bf16[128,2048]{1,0:T(8,128)(2,1)S(1)} %copy-done.6, bf16[128,4096]{0,1:T(8,128)(2,1)} %all-gather.27.cloned.1.call-done, bf16[1,4096,2048]{2,1,0:T(8,128)(2,1)} %param.11), kind=kOutput, calls=%fused_computation.164 | convolution fusion | flops 2148270080 | bytes 18874368 | tf_op jit(solution)/shard_map/dot_general | solution.py:75
  255.5 3.4 collective-permute-start.2
  258.9 11.5 %collective-permute-done.2 = bf16[128,2048]{1,0:T(8,128)(2,1)S(1)} collective-permute-done((bf16[128,2048]{1,0:T(8,128)(2,1)S(1)}, bf16[128,2048]{1,0:T(8,128)(2,1)S(1)}, u32[]{:S(2)}, u32[]{:S(2)}) %collective-permute-start.2) | collective-permute-done | bytes 524320 | tf_op jit(solution)/shard_map/ppermute | solution.py:24
  272.9 22.2 %all-gather.29.cloned.1.call-done = bf16[128,8192]{1,0:T(8,128)(2,1)} async-done(((bf16[128,2048]{1,0:T(8,128)(2,1)}), bf16[128,8192]{1,0:T(8,128)(2,1)}) %all-gather.29.cloned.1.call-update) | async-done | bytes 2097168 | tf_op jit(solution)/shard_map/all_gather | solution.py:85
  295.1 2.2 fusion.58
  297.3 8.2 %fusion.99 = bf16[128,1024]{1,0:T(8,128)(2,1)S(1)} fusion(bf16[1,8192,1024]{2,1,0:T(8,128)(2,1)} %param.9, bf16[128,8192]{1,0:T(8,128)(2,1)S(1)} %copy-done.10, f32[128]{0:T(128)S(1)} %add_rsqrt_fusion.3, f32[8192]{0:T(1024)S(1)} %bitcast.390), kind=kOutput, calls=%fused_computation.127 | convolution fusion | flops 2151809024 | bytes 19169792 | tf_op jit(solution)/shard_map/dot_general | solution.py:70
  306.5 5.3 fusion.153
  314.9 2.0 fusion.329
  316.9 3.0 convolution_convert_fusion.4
  320.0 16.8 %all-gather.31.cloned.1.call-done = bf16[128,4096]{0,1:T(8,128)(2,1)} async-done(((bf16[128,1024]{0,1:T(8,128)(2,1)}), bf16[128,4096]{0,1:T(8,128)(2,1)}) %all-gather.31.cloned.1.call-update) | async-done | bytes 1048592 | tf_op jit(solution)/shard_map/all_gather | solution.py:129
  336.8 8.5 %add_convert_fusion.3 = bf16[128,2048]{1,0:T(8,128)(2,1)S(1)} fusion(bf16[128,2048]{1,0:T(8,128)(2,1)S(1)} %copy-done.4, bf16[128,4096]{0,1:T(8,128)(2,1)} %all-gather.31.cloned.1.call-done, bf16[1,4096,2048]{2,1,0:T(8,128)(2,1)} %param.11), kind=kOutput, calls=%fused_computation.155 | convolution fusion | flops 2148270080 | bytes 18874368 | tf_op jit(solution)/shard_map/dot_general | solution.py:75
  346.1 3.5 collective-permute-start.3
  349.6 11.5 %collective-permute-done.3 = bf16[128,2048]{1,0:T(8,128)(2,1)S(1)} collective-permute-done((bf16[128,2048]{1,0:T(8,128)(2,1)S(1)}, bf16[128,2048]{1,0:T(8,128)(2,1)S(1)}, u32[]{:S(2)}, u32[]{:S(2)}) %collective-permute-start.3) | collective-permute-done | bytes 524320 | tf_op jit(solution)/shard_map/ppermute | solution.py:24
  362.3 23.5 %all-gather.33.cloned.1.call-done = bf16[128,8192]{1,0:T(8,128)(2,1)} async-done(((bf16[128,2048]{1,0:T(8,128)(2,1)}), bf16[128,8192]{1,0:T(8,128)(2,1)}) %all-gather.33.cloned.1.call-update) | async-done | bytes 2097168 | tf_op jit(solution)/shard_map/all_gather | solution.py:85
  385.8 2.2 fusion.61
  388.1 8.2 %fusion.102 = bf16[128,1024]{1,0:T(8,128)(2,1)S(1)} fusion(bf16[1,8192,1024]{2,1,0:T(8,128)(2,1)} %param.9, bf16[128,8192]{1,0:T(8,128)(2,1)S(1)} %copy-done.14, f32[128]{0:T(128)S(1)} %add_rsqrt_fusion.2, f32[8192]{0:T(1024)S(1)} %bitcast.392), kind=kOutput, calls=%fused_computation.128 | convolution fusion | flops 2151809024 | bytes 19169792 | tf_op jit(solution)/shard_map/dot_general | solution.py:70
  397.2 5.3 fusion.147
  407.6 3.0 convolution_convert_fusion.3
  410.7 16.8 %all-gather.35.cloned.1.call-done = bf16[128,4096]{0,1:T(8,128)(2,1)} async-done(((bf16[128,1024]{0,1:T(8,128)(2,1)}), bf16[128,4096]{0,1:T(8,128)(2,1)}) %all-gather.35.cloned.1.call-update) | async-done | bytes 1048592 | tf_op jit(solution)/shard_map/all_gather | solution.py:129
  427.5 8.5 %add_convert_fusion.2 = bf16[128,2048]{1,0:T(8,128)(2,1)S(1)} fusion(bf16[128,2048]{1,0:T(8,128)(2,1)S(1)} %copy-done.7, bf16[128,4096]{0,1:T(8,128)(2,1)} %all-gather.35.cloned.1.call-done, bf16[1,4096,2048]{2,1,0:T(8,128)(2,1)} %param.11), kind=kOutput, calls=%fused_computation.154 | convolution fusion | flops 2148270080 | bytes 18874368 | tf_op jit(solution)/shard_map/dot_general | solution.py:75
  436.8 3.5 collective-permute-start.4
  440.3 11.5 %collective-permute-done.4 = bf16[128,2048]{1,0:T(8,128)(2,1)S(1)} collective-permute-done((bf16[128,2048]{1,0:T(8,128)(2,1)S(1)}, bf16[128,2048]{1,0:T(8,128)(2,1)S(1)}, u32[]{:S(2)}, u32[]{:S(2)}) %collective-permute-start.4) | collective-permute-done | bytes 524320 | tf_op jit(solution)/shard_map/ppermute | solution.py:24
  453.0 23.4 %all-gather.37.cloned.1.call-done = bf16[128,8192]{1,0:T(8,128)(2,1)} async-done(((bf16[128,2048]{1,0:T(8,128)(2,1)}), bf16[128,8192]{1,0:T(8,128)(2,1)}) %all-gather.37.cloned.1.call-update) | async-done | bytes 2097168 | tf_op jit(solution)/shard_map/all_gather | solution.py:85
  476.5 2.2 fusion.64
  478.7 8.3 %fusion.105 = bf16[128,1024]{1,0:T(8,128)(2,1)S(1)} fusion(bf16[1,8192,1024]{2,1,0:T(8,128)(2,1)} %param.9, bf16[128,8192]{1,0:T(8,128)(2,1)S(1)} %copy-done.15, f32[128]{0:T(128)S(1)} %add_rsqrt_fusion.1, f32[8192]{0:T(1024)S(1)} %bitcast.394), kind=kOutput, calls=%fused_computation.129 | convolution fusion | flops 2151809024 | bytes 19169792 | tf_op jit(solution)/shard_map/dot_general | solution.py:70
  487.9 5.3 fusion.141
  498.3 3.0 convolution_convert_fusion.2
  501.3 16.8 %all-gather.39.cloned.1.call-done = bf16[128,4096]{0,1:T(8,128)(2,1)} async-done(((bf16[128,1024]{0,1:T(8,128)(2,1)}), bf16[128,4096]{0,1:T(8,128)(2,1)}) %all-gather.39.cloned.1.call-update) | async-done | bytes 1048592 | tf_op jit(solution)/shard_map/all_gather | solution.py:129
  518.1 8.5 %add_convert_fusion.1 = bf16[128,2048]{1,0:T(8,128)(2,1)S(1)} fusion(bf16[128,2048]{1,0:T(8,128)(2,1)S(1)} %copy-done.8, bf16[128,4096]{0,1:T(8,128)(2,1)} %all-gather.39.cloned.1.call-done, bf16[1,4096,2048]{2,1,0:T(8,128)(2,1)} %param.11), kind=kOutput, calls=%fused_computation.153 | convolution fusion | flops 2148270080 | bytes 18874368 | tf_op jit(solution)/shard_map/dot_general | solution.py:75
  527.4 3.5 collective-permute-start.5
  531.0 11.5 %collective-permute-done.5 = bf16[128,2048]{1,0:T(8,128)(2,1)S(1)} collective-permute-done((bf16[128,2048]{1,0:T(8,128)(2,1)S(1)}, bf16[128,2048]{1,0:T(8,128)(2,1)S(1)}, u32[]{:S(2)}, u32[]{:S(2)}) %collective-permute-start.5) | collective-permute-done | bytes 524320 | tf_op jit(solution)/shard_map/ppermute | solution.py:24
  543.7 23.4 %all-gather.41.cloned.1.call-done = bf16[128,8192]{1,0:T(8,128)(2,1)} async-done(((bf16[128,2048]{1,0:T(8,128)(2,1)}), bf16[128,8192]{1,0:T(8,128)(2,1)}) %all-gather.41.cloned.1.call-update) | async-done | bytes 2097168 | tf_op jit(solution)/shard_map/all_gather | solution.py:85
  567.1 2.2 fusion.67
  569.4 8.1 %fusion.108 = bf16[128,1024]{1,0:T(8,128)(2,1)S(1)} fusion(bf16[1,8192,1024]{2,1,0:T(8,128)(2,1)} %param.9, bf16[128,8192]{1,0:T(8,128)(2,1)S(1)} %copy-done.13, f32[128]{0:T(128)S(1)} %add_rsqrt_fusion, f32[8192]{0:T(1024)S(1)} %bitcast.396), kind=kOutput, calls=%fused_computation.130 | convolution fusion | flops 2151809024 | bytes 19169792 | tf_op jit(solution)/shard_map/dot_general | solution.py:70
  577.7 4.7 fusion.135
  591.3 12.3 %all-gather.43.cloned.1.call-done = bf16[128,4096]{0,1:T(8,128)(2,1)} async-done(((bf16[128,1024]{0,1:T(8,128)(2,1)}), bf16[128,4096]{0,1:T(8,128)(2,1)}) %all-gather.43.cloned.1.call-update) | async-done | bytes 1048592 | tf_op jit(solution)/shard_map/all_gather | solution.py:129
  603.6 8.5 %fusion.7 = f32[128,2048]{1,0:T(8,128)S(1)} fusion(bf16[128,4096]{0,1:T(8,128)(2,1)} %all-gather.43.cloned.1.call-done, bf16[1,4096,2048]{2,1,0:T(8,128)(2,1)} %param.11), kind=kOutput, calls=%fused_computation.7 | convolution fusion | flops 2147483648 | bytes 18874368 | tf_op jit(solution)/shard_map/dot_general | solution.py:75
  613.2 14.4 %all-gather.45.cloned.1.call-done = bf16[2048,512]{1,0:T(8,128)(2,1)} async-done(((bf16[512,512]{1,0:T(8,128)(2,1)}), bf16[2048,512]{1,0:T(8,128)(2,1)}) %all-gather.45.cloned.1.call-update) | async-done | bytes 2097168 | tf_op jit(solution)/shard_map/all_gather | solution.py:31
  627.6 2.5 reshape.520
  (171 shorter events, 54.1 us)
Async XLA Ops:
  7.2 28.3 %all-gather.17.cloned.1.call-start = ((), (), s32[]{:S(2)}) async-start(), calls=%async_computation | async-start | bytes 2621440 | tf_op jit(solution)/shard_map/all_gather | solution.py:85
  9.2 60.2 %all-gather.19.cloned.1.call-start = ((), (), s32[]{:S(2)}) async-start(), calls=%async_computation.1 | async-start | bytes 1310720 | tf_op jit(solution)/shard_map/all_gather | solution.py:129
  15.8 201.0 %copy-start.25 = (f32[1,8192]{1,0:T(1,128)}, f32[1,8192]{1,0:T(1,128)S(1)}, u32[]{:S(2)}) copy-start(f32[1,8192]{1,0:T(1,128)S(1)} %mul.257) | copy-start | bytes 98308
  35.4 2.2 copy-start.9
  50.9 18.5 %copy-start.2 = (bf16[128,2048]{1,0:T(8,128)(2,1)S(1)}, bf16[128,2048]{1,0:T(8,128)(2,1)}, u32[]{:S(2)}) copy-start(bf16[128,2048]{1,0:T(8,128)(2,1)} %dynamic-slice_select_fusion) | copy-start | bytes 1572868
  52.6 40.3 %copy-start.1 = (bf16[512,2048]{1,0:T(8,128)(2,1)S(1)}, bf16[512,2048]{1,0:T(8,128)(2,1)}, u32[]{:S(2)}) copy-start(bf16[512,2048]{1,0:T(8,128)(2,1)} %param.7) | copy-start | bytes 6291460
  52.6 64.9 %all-gather.21.cloned.1.call-start = ((), (), s32[]{:S(2)}) async-start(), calls=%async_computation.2 | async-start | bytes 2621440 | tf_op jit(solution)/shard_map/all_gather | solution.py:85
  77.9 16.2 %slice-start = ((s32[512]{0:T(512)}), s32[256]{0:T(256)S(1)}, s32[]{:S(2)}) async-start(s32[512]{0:T(512)} %param.13), calls=%async_computation.15 | async-start | bytes 2048 | tf_op jit(solution)/shard_map/slice | solution.py:119
  77.9 15.0 %collective-permute-start = (bf16[128,2048]{1,0:T(8,128)(2,1)S(1)}, bf16[128,2048]{1,0:T(8,128)(2,1)S(1)}, u32[]{:S(2)}, u32[]{:S(2)}) collective-permute-start(bf16[128,2048]{1,0:T(8,128)(2,1)S(1)} %fusion.73), channel_id=1, source_target_pairs={{0,1},{1,2},{2,3},{4,5},{5,6},{6,7},{8,9},{9,10},{10,11},{12,13},{... | collective-permute-start | bytes 1572872 | tf_op jit(solution)/shard_map/ppermute | solution.py:24
  93.8 63.5 %all-gather.23.cloned.1.call-start = ((), (), s32[]{:S(2)}) async-start(), calls=%async_computation.3 | async-start | bytes 1310720 | tf_op jit(solution)/shard_map/all_gather | solution.py:129
  117.5 2.2 copy-start.11
  134.7 1.5 copy-start.16
  137.7 19.6 %copy-start.5 = (bf16[128,2048]{1,0:T(8,128)(2,1)S(1)}, bf16[128,2048]{1,0:T(8,128)(2,1)}, u32[]{:S(2)}) copy-start(bf16[128,2048]{1,0:T(8,128)(2,1)} %dynamic-slice_select_fusion.1) | copy-start | bytes 1572868
  140.4 64.9 %all-gather.25.cloned.1.call-start = ((), (), s32[]{:S(2)}) async-start(), calls=%async_computation.4 | async-start | bytes 2621440 | tf_op jit(solution)/shard_map/all_gather | solution.py:85
  165.8 16.2 %copy-start.24 = (s32[512]{0:T(512)S(1)}, s32[512]{0:T(512)}, u32[]{:S(2)}) copy-start(s32[512]{0:T(512)} %param.13) | copy-start | bytes 6148
  165.8 15.0 %collective-permute-start.1 = (bf16[128,2048]{1,0:T(8,128)(2,1)S(1)}, bf16[128,2048]{1,0:T(8,128)(2,1)S(1)}, u32[]{:S(2)}, u32[]{:S(2)}) collective-permute-start(bf16[128,2048]{1,0:T(8,128)(2,1)S(1)} %add_convert_fusion.5), channel_id=1, source_target_pairs={{0,1},{1,2},{2,3},{4,5},{5,6},{6,7},{8,9},{9,10},{10,11},{12,13},{... | collective-permute-start | bytes 1572872 | tf_op jit(solution)/shard_map/ppermute | solution.py:24
  181.7 65.3 %all-gather.27.cloned.1.call-start = ((), (), s32[]{:S(2)}) async-start(), calls=%async_computation.5 | async-start | bytes 1310720 | tf_op jit(solution)/shard_map/all_gather | solution.py:129
  205.4 2.2 copy-start.12
  224.7 2.9 copy-start.23
  227.6 19.4 %copy-start.6 = (bf16[128,2048]{1,0:T(8,128)(2,1)S(1)}, bf16[128,2048]{1,0:T(8,128)(2,1)}, u32[]{:S(2)}) copy-start(bf16[128,2048]{1,0:T(8,128)(2,1)} %dynamic-slice_select_fusion.2) | copy-start | bytes 1572868
  230.1 65.0 %all-gather.29.cloned.1.call-start = ((), (), s32[]{:S(2)}) async-start(), calls=%async_computation.6 | async-start | bytes 2621440 | tf_op jit(solution)/shard_map/all_gather | solution.py:85
  255.5 16.5 %copy-start.30 = (s32[128]{0:T(128)S(1)}, s32[128]{0:T(128)}, u32[]{:S(2)}) copy-start(s32[128]{0:T(128)} %get-tuple-element.25) | copy-start | bytes 1540
  255.5 41.9 %copy-start.26 = (f32[1,8192]{1,0:T(1,128)S(1)}, f32[1,8192]{1,0:T(1,128)}, u32[]{:S(2)}) copy-start(f32[1,8192]{1,0:T(1,128)} %copy-done.25) | copy-start | bytes 98308
  255.5 14.9 %collective-permute-start.2 = (bf16[128,2048]{1,0:T(8,128)(2,1)S(1)}, bf16[128,2048]{1,0:T(8,128)(2,1)S(1)}, u32[]{:S(2)}, u32[]{:S(2)}) collective-permute-start(bf16[128,2048]{1,0:T(8,128)(2,1)S(1)} %add_convert_fusion.4), channel_id=1, source_target_pairs={{0,1},{1,2},{2,3},{4,5},{5,6},{6,7},{8,9},{9,10},{10,11},{12,13},{... | collective-permute-start | bytes 1572872 | tf_op jit(solution)/shard_map/ppermute | solution.py:24
  271.4 65.4 %all-gather.31.cloned.1.call-start = ((), (), s32[]{:S(2)}) async-start(), calls=%async_computation.7 | async-start | bytes 1310720 | tf_op jit(solution)/shard_map/all_gather | solution.py:129
  295.1 2.3 copy-start.10
  316.9 19.9 %copy-start.4 = (bf16[128,2048]{1,0:T(8,128)(2,1)S(1)}, bf16[128,2048]{1,0:T(8,128)(2,1)}, u32[]{:S(2)}) copy-start(bf16[128,2048]{1,0:T(8,128)(2,1)} %dynamic-slice_select_fusion.3) | copy-start | bytes 1572868
  319.9 65.9 %all-gather.33.cloned.1.call-start = ((), (), s32[]{:S(2)}) async-start(), calls=%async_computation.8 | async-start | bytes 2621440 | tf_op jit(solution)/shard_map/all_gather | solution.py:85
  345.3 0.8 copy-start.17
  346.1 42.0 %copy-start.27 = (f32[1,8192]{1,0:T(1,128)S(1)}, f32[1,8192]{1,0:T(1,128)}, u32[]{:S(2)}) copy-start(f32[1,8192]{1,0:T(1,128)} %copy-done.25) | copy-start | bytes 98308
  346.1 15.1 %collective-permute-start.3 = (bf16[128,2048]{1,0:T(8,128)(2,1)S(1)}, bf16[128,2048]{1,0:T(8,128)(2,1)S(1)}, u32[]{:S(2)}, u32[]{:S(2)}) collective-permute-start(bf16[128,2048]{1,0:T(8,128)(2,1)S(1)} %add_convert_fusion.3), channel_id=1, source_target_pairs={{0,1},{1,2},{2,3},{4,5},{5,6},{6,7},{8,9},{9,10},{10,11},{12,13},{... | collective-permute-start | bytes 1572872 | tf_op jit(solution)/shard_map/ppermute | solution.py:24
  362.1 65.4 %all-gather.35.cloned.1.call-start = ((), (), s32[]{:S(2)}) async-start(), calls=%async_computation.9 | async-start | bytes 1310720 | tf_op jit(solution)/shard_map/all_gather | solution.py:129
  385.8 2.3 copy-start.14
  407.6 19.9 %copy-start.7 = (bf16[128,2048]{1,0:T(8,128)(2,1)S(1)}, bf16[128,2048]{1,0:T(8,128)(2,1)}, u32[]{:S(2)}) copy-start(bf16[128,2048]{1,0:T(8,128)(2,1)} %dynamic-slice_select_fusion.4) | copy-start | bytes 1572868
  410.6 65.9 %all-gather.37.cloned.1.call-start = ((), (), s32[]{:S(2)}) async-start(), calls=%async_computation.10 | async-start | bytes 2621440 | tf_op jit(solution)/shard_map/all_gather | solution.py:85
  436.0 0.8 copy-start.19
  436.8 42.0 %copy-start.28 = (f32[1,8192]{1,0:T(1,128)S(1)}, f32[1,8192]{1,0:T(1,128)}, u32[]{:S(2)}) copy-start(f32[1,8192]{1,0:T(1,128)} %copy-done.25) | copy-start | bytes 98308
  436.8 15.1 %collective-permute-start.4 = (bf16[128,2048]{1,0:T(8,128)(2,1)S(1)}, bf16[128,2048]{1,0:T(8,128)(2,1)S(1)}, u32[]{:S(2)}, u32[]{:S(2)}) collective-permute-start(bf16[128,2048]{1,0:T(8,128)(2,1)S(1)} %add_convert_fusion.2), channel_id=1, source_target_pairs={{0,1},{1,2},{2,3},{4,5},{5,6},{6,7},{8,9},{9,10},{10,11},{12,13},{... | collective-permute-start | bytes 1572872 | tf_op jit(solution)/shard_map/ppermute | solution.py:24
  452.8 65.4 %all-gather.39.cloned.1.call-start = ((), (), s32[]{:S(2)}) async-start(), calls=%async_computation.11 | async-start | bytes 1310720 | tf_op jit(solution)/shard_map/all_gather | solution.py:129
  476.5 2.3 copy-start.15
  498.3 19.9 %copy-start.8 = (bf16[128,2048]{1,0:T(8,128)(2,1)S(1)}, bf16[128,2048]{1,0:T(8,128)(2,1)}, u32[]{:S(2)}) copy-start(bf16[128,2048]{1,0:T(8,128)(2,1)} %dynamic-slice_select_fusion.5) | copy-start | bytes 1572868
  501.3 65.8 %all-gather.41.cloned.1.call-start = ((), (), s32[]{:S(2)}) async-start(), calls=%async_computation.12 | async-start | bytes 2621440 | tf_op jit(solution)/shard_map/all_gather | solution.py:85
  526.6 0.8 copy-start.21
  527.4 42.0 %copy-start.29 = (f32[1,8192]{1,0:T(1,128)S(1)}, f32[1,8192]{1,0:T(1,128)}, u32[]{:S(2)}) copy-start(f32[1,8192]{1,0:T(1,128)} %copy-done.25) | copy-start | bytes 98308
  527.4 15.1 %collective-permute-start.5 = (bf16[128,2048]{1,0:T(8,128)(2,1)S(1)}, bf16[128,2048]{1,0:T(8,128)(2,1)S(1)}, u32[]{:S(2)}, u32[]{:S(2)}) collective-permute-start(bf16[128,2048]{1,0:T(8,128)(2,1)S(1)} %add_convert_fusion.1), channel_id=1, source_target_pairs={{0,1},{1,2},{2,3},{4,5},{5,6},{6,7},{8,9},{9,10},{10,11},{12,13},{... | collective-permute-start | bytes 1572872 | tf_op jit(solution)/shard_map/ppermute | solution.py:24
  543.4 60.2 %all-gather.43.cloned.1.call-start = ((), (), s32[]{:S(2)}) async-start(), calls=%async_computation.13 | async-start | bytes 1310720 | tf_op jit(solution)/shard_map/all_gather | solution.py:129
  567.1 2.3 copy-start.13
  582.4 2.4 copy-start
  584.9 2.5 copy-start.18
  584.9 3.9 copy-start.20
  584.9 4.6 copy-start.22
  586.7 40.9 %all-gather.45.cloned.1.call-start = ((), (), s32[]{:S(2)}) async-start(), calls=%async_computation.14 | async-start | bytes 2621440 | tf_op jit(solution)/shard_map/all_gather | solution.py:31
  587.4 24.7 %copy-start.3 = (bf16[128,2048]{1,0:T(8,128)(2,1)S(1)}, bf16[128,2048]{1,0:T(8,128)(2,1)}, u32[]{:S(2)}) copy-start(bf16[128,2048]{1,0:T(8,128)(2,1)} %dynamic-slice_select_fusion.6) | copy-start | bytes 1572868
  587.4 24.7 %collective-permute-start.8 = (bf16[128,2048]{1,0:T(8,128)(2,1)S(1)}, bf16[128,2048]{1,0:T(8,128)(2,1)S(1)}, u32[]{:S(2)}, u32[]{:S(2)}) collective-permute-start(bf16[128,2048]{1,0:T(8,128)(2,1)S(1)} %copy-done.18), channel_id=1, source_target_pairs={{3,0},{7,4},{11,8},{15,12},{19,16},{23,20},{27,24},{31,28}} | collective-permute-start | bytes 1572872 | tf_op jit(solution)/shard_map/ppermute | solution.py:135
  588.8 23.3 %collective-permute-start.7 = (bf16[128,2048]{1,0:T(8,128)(2,1)S(1)}, bf16[128,2048]{1,0:T(8,128)(2,1)S(1)}, u32[]{:S(2)}, u32[]{:S(2)}) collective-permute-start(bf16[128,2048]{1,0:T(8,128)(2,1)S(1)} %copy-done.20), channel_id=1, source_target_pairs={{3,1},{7,5},{11,9},{15,13},{19,17},{23,21},{27,25},{31,29}} | collective-permute-start | bytes 1572872 | tf_op jit(solution)/shard_map/ppermute | solution.py:135
  589.5 22.6 %collective-permute-start.6 = (bf16[128,2048]{1,0:T(8,128)(2,1)S(1)}, bf16[128,2048]{1,0:T(8,128)(2,1)}, u32[]{:S(2)}, u32[]{:S(2)}) collective-permute-start(bf16[128,2048]{1,0:T(8,128)(2,1)S(1)} %copy-done.22), channel_id=1, source_target_pairs={{3,2},{7,6},{11,10},{15,14},{19,18},{23,22},{27,26},{31,30}} | collective-permute-start | bytes 1572872 | tf_op jit(solution)/shard_map/ppermute | solution.py:135
  631.0 0.7 copy-start.31
Sparse Core Ops, SparseCore 0:
  10.1 25.2 all-gather.16
  52.7 16.6 all-gather.18
  93.9 23.5 all-gather.20
  140.6 16.6 all-gather.22
  181.8 23.5 all-gather.24
  230.2 16.6 all-gather.26
  271.5 23.5 all-gather.28
  320.0 16.7 all-gather.30
  362.2 23.5 all-gather.32
  410.7 16.6 all-gather.34
  452.9 23.5 all-gather.36
  501.4 16.6 all-gather.38
  543.5 23.5 all-gather.40
  586.8 16.6 all-gather.42
  605.0 22.5 all-gather.44
